TPU v7x, 128 devices: a whole 4x4x4 slice. The times are simulated.
128 devices in a mesh: south: 2 (over x_hi), east: 8 (over y, core), down: 8 (over z, x_lo).
Axes of the slice: x: 4 (x_hi: 2, x_lo: 2; x = x_hi * 2 + x_lo), y: 4, z: 4, core: 2. Of those that a mesh axis runs over, the one named last changes fastest.
Arguments:
- field_values: float32 [256, 64, 64, 128], P('south', 'east', 'down'), may hold values from 0.5 to 2
- flow_j: float32 [256, 64, 64, 128], P('south', 'east', 'down'), may hold values from -0.3 to 0.3
- flow_i: float32 [256, 64, 64, 128], P('south', 'east', 'down'), may hold values from -0.3 to 0.3
- flow_k: float32 [256, 64, 64, 128], P('south', 'east', 'down'), may hold values from -0.3 to 0.3
Outputs:
- standardized: float32 [256, 64, 64, 128], P('south', 'east', 'down')
- field_values_end: float32 [256, 64, 64, 128], P('south', 'east', 'down')
All inputs are finite; a program needn't handle non-finite values.
Results may differ from a plain program's by a relative error of at most 0.00002.
Values sent between devices are 32-bit elements; how exact they have to be, the bound alone decides.
A program may use at most 128 MiB of HBM per device.

v0:
```python
import jax
import jax.numpy as jnp
from jax import lax
from jax.sharding import PartitionSpec as P

STEPS = 6


def with_halo(shard, sides, width):
    edges = {}
    for axis, dim in sides:
        devices, length = (lax.axis_size(axis), shard.shape[dim])
        up = [(i, (i + 1) % devices) for i in range(devices - 1)]
        last = lax.slice_in_dim(shard, length - width, length, axis=dim)
        leading = lax.slice_in_dim(shard, 0, width, axis=dim)
        edges[dim] = (
            lax.ppermute(last, axis, up),
            lax.ppermute(leading, axis, [(b, a) for a, b in up]),
        )
    done = []
    for _, dim in sides:
        low, high = edges[dim]
        around = [(width, width) if d in done else (0, 0) for d in range(shard.ndim)]
        shard = jnp.concatenate([jnp.pad(low, around), shard, jnp.pad(high, around)], axis=dim)
        done.append(dim)
    return shard


def sent_to_all(shard, axis):
    devices = lax.axis_size(axis)
    return lax.all_to_all(
        jnp.broadcast_to(shard[None], (devices, *shard.shape)), axis, 0, 0, tiled=True
    )


def taken_together(shard, axis):
    everything = sent_to_all(shard, axis)
    return jnp.sum(everything, axis=0)


def in_one(arrays, axis):
    ends = [0]
    for a in arrays:
        ends.append(ends[-1] + a.size)
    total = taken_together(jnp.concatenate([a.ravel() for a in arrays]), axis)
    return tuple((total[b:e].reshape(a.shape) for a, b, e in zip(arrays, ends, ends[1:])))


def inner_cells(values, dims):
    for dim in dims:
        values = lax.slice_in_dim(values, 1, values.shape[dim] - 1, axis=dim)
    return values


def side_cells(values, dim, start, dims):
    others = [other for other in dims if other != dim]
    values = inner_cells(values, others)
    return lax.slice_in_dim(values, start, start + values.shape[dim] - 2, axis=dim)


def advance(padded, flow_j, flow_i, flow_k):
    middle = inner_cells(padded, (0, 1, 2))
    lower = [side_cells(padded, dim, 0, (0, 1, 2)) for dim in (0, 1, 2)]
    upper = [side_cells(padded, dim, 2, (0, 1, 2)) for dim in (0, 1, 2)]
    slopes = [above - below for above, below in zip(upper, lower)]
    smooth_rate = 0.05
    spread = lower[0] + upper[0] + lower[1] + upper[1] + lower[2] + upper[2] - 6.0 * middle
    return (
        middle - flow_j * slopes[0] - flow_i * slopes[1] - flow_k * slopes[2] + smooth_rate * spread
    )


def per_device(field_values, flow_j, flow_i, flow_k):
    for step in range(STEPS):
        padded = with_halo(field_values, (("south", 0), ("east", 1), ("down", 2)), 1)
        field_values = advance(padded, flow_j, flow_i, flow_k)
    count = field_values.shape[0] * lax.axis_size("south")
    guess = 1.0
    moved = field_values - guess
    totals, squares = in_one(
        (jnp.sum(moved, axis=0, keepdims=True), jnp.sum(moved * moved, axis=0, keepdims=True)),
        "south",
    )
    line_mean = guess + totals / count
    centred = field_values - line_mean
    line_variance = squares / count - totals / count * (totals / count)
    standardized = centred * lax.rsqrt(line_variance + 0.0001)
    return (standardized, field_values)


def solution(mesh):
    return jax.shard_map(
        per_device,
        mesh=mesh,
        in_specs=(
            P("south", "east", "down", None),
            P("south", "east", "down", None),
            P("south", "east", "down", None),
            P("south", "east", "down", None),
        ),
        out_specs=(P("south", "east", "down", None), P("south", "east", "down", None)),
        check_vma=False,
    )
```

profile of v0, /device:TPU:96, one launch (start us, length us, event | category | flops | bytes accessed | tf_op | source)
XLA Modules:
  0.0 293.4 jit_solution(18436670900424788471)
XLA Ops:
  1.9 1.3 collective-permute-start.2
  3.2 3.1 %collective-permute-start.3 = (f32[128,1,8,128]{3,2,1,0:T(8,128)S(1)}, f32[128,1,8,128]{3,2,1,0:T(8,128)S(1)}, u32[]{:S(2)}, u32[]{:S(2)}) collective-permute-start(f32[128,1,8,128]{3,2,1,0:T(8,128)S(1)} %get-tuple-element.41), channel_id=1, source_target_pairs={{0,8},{8,16},{16,24},{24,32},{32,40},{40,48},{48,56},{1,9},{9,17},... | collective-permute-start | bytes 1572872 | tf_op jit(solution)/shard_map/ppermute | solution.py:17
  6.3 4.7 %fusion.31 = (f32[128,8,1,128]{3,2,1,0:T(1,128)S(1)}, f32[128,8,1,128]{3,2,1,0:T(1,128)S(1)}) fusion(f32[128,8,8,128]{3,2,1,0:T(8,128)} %param.4), kind=kLoop, calls=%fused_computation.149 | loop fusion | bytes 2097152 | tf_op jit(solution)/shard_map/slice | solution.py:14
  11.0 3.2 %collective-permute-start.4 = (f32[128,8,1,128]{3,1,2,0:T(8,128)S(1)}, f32[128,8,1,128]{3,1,2,0:T(8,128)}, u32[]{:S(2)}, u32[]{:S(2)}) collective-permute-start(f32[128,8,1,128]{3,1,2,0:T(8,128)S(1)} %bitcast.46), channel_id=1, source_target_pairs={{1,0},{2,1},{3,2},{4,3},{5,4},{6,5},{7,6},{9,8},{10,9},{11,10},{12... | collective-permute-start | bytes 1572872 | tf_op jit(solution)/shard_map/ppermute | solution.py:18
  14.3 3.4 %collective-permute-start.5 = (f32[128,8,1,128]{3,1,2,0:T(8,128)S(1)}, f32[128,8,1,128]{3,1,2,0:T(8,128)}, u32[]{:S(2)}, u32[]{:S(2)}) collective-permute-start(f32[128,8,1,128]{3,1,2,0:T(8,128)S(1)} %bitcast.40), channel_id=1, source_target_pairs={{0,1},{1,2},{2,3},{3,4},{4,5},{5,6},{6,7},{8,9},{9,10},{10,11},{11... | collective-permute-start | bytes 1572872 | tf_op jit(solution)/shard_map/ppermute | solution.py:17
  18.5 4.9 %collective-permute-start.1 = (f32[1,8,8,128]{3,2,1,0:T(8,128)S(1)}, f32[1,8,8,128]{3,2,1,0:T(8,128)S(1)}, u32[]{:S(2)}, u32[]{:S(2)}) collective-permute-start(f32[1,8,8,128]{3,2,1,0:T(8,128)S(1)} %get-tuple-element.44), channel_id=1, source_target_pairs={{0,64},{1,65},{2,66},{3,67},{4,68},{5,69},{6,70},{7,71},{8,72},{9,... | collective-permute-start | bytes 98312 | tf_op jit(solution)/shard_map/ppermute | solution.py:17
  23.4 14.9 %collective-permute-done.1 = f32[1,8,8,128]{3,2,1,0:T(8,128)S(1)} collective-permute-done((f32[1,8,8,128]{3,2,1,0:T(8,128)S(1)}, f32[1,8,8,128]{3,2,1,0:T(8,128)S(1)}, u32[]{:S(2)}, u32[]{:S(2)}) %collective-permute-start.1) | collective-permute-done | bytes 32800 | tf_op jit(solution)/shard_map/ppermute | solution.py:17
  39.6 2.7 constant_dynamic-update-slice_fusion.1
  42.3 3.3 %collective-permute-done = f32[1,8,8,128]{3,2,1,0:T(8,128)S(1)} collective-permute-done((f32[1,8,8,128]{3,2,1,0:T(8,128)S(1)}, f32[1,8,8,128]{3,2,1,0:T(8,128)S(1)}, u32[]{:S(2)}, u32[]{:S(2)}) %collective-permute-start) | collective-permute-done | bytes 32800 | tf_op jit(solution)/shard_map/ppermute | solution.py:18
  45.8 11.9 %multiply_add_fusion.5 = f32[128,8,8,128]{3,2,1,0:T(8,128)S(1)} fusion(f32[128,8,8,128]{3,2,1,0:T(8,128)} %param.4, f32[128,8,8,128]{3,2,1,0:T(8,128)S(1)} %copy-done, f32[128,8,1,128]{3,2,1,0:T(1,128)} %bitcast.25, f32[130,1,8,128]{3,2,1,0:T(8,128)S(1)} %pad.74, f32[130,8,8,128]{3,2,1,0:T(8,128)S(1)} %constant_dynamic-update-slice_fusion, ...), kind=kLoop, calls=%fused_computation.121 | loop fusion | flops 35651584 | bytes 27410432 | tf_op jit(solution)/shard_map/add | solution.py:69
  57.7 1.3 collective-permute-start.8
  59.7 3.1 %collective-permute-start.9 = (f32[128,1,8,128]{3,2,1,0:T(8,128)S(1)}, f32[128,1,8,128]{3,2,1,0:T(8,128)S(1)}, u32[]{:S(2)}, u32[]{:S(2)}) collective-permute-start(f32[128,1,8,128]{3,2,1,0:T(8,128)S(1)} %get-tuple-element.35), channel_id=1, source_target_pairs={{0,8},{8,16},{16,24},{24,32},{32,40},{40,48},{48,56},{1,9},{9,17},... | collective-permute-start | bytes 1572872 | tf_op jit(solution)/shard_map/ppermute | solution.py:17
  62.8 2.4 collective-permute-start.10
  65.2 3.4 %collective-permute-start.11 = (f32[128,8,1,128]{3,1,2,0:T(8,128)S(1)}, f32[128,8,1,128]{3,1,2,0:T(8,128)S(1)}, u32[]{:S(2)}, u32[]{:S(2)}) collective-permute-start(f32[128,8,1,128]{3,1,2,0:T(8,128)S(1)} %bitcast.41), channel_id=1, source_target_pairs={{0,1},{1,2},{2,3},{3,4},{4,5},{5,6},{6,7},{8,9},{9,10},{10,11},{11... | collective-permute-start | bytes 1572872 | tf_op jit(solution)/shard_map/ppermute | solution.py:17
  68.7 1.3 collective-permute-start.6
  70.0 6.0 %collective-permute-start.7 = (f32[1,8,8,128]{3,2,1,0:T(8,128)S(1)}, f32[1,8,8,128]{3,2,1,0:T(8,128)S(1)}, u32[]{:S(2)}, u32[]{:S(2)}) collective-permute-start(f32[1,8,8,128]{3,2,1,0:T(8,128)S(1)} %get-tuple-element.37), channel_id=1, source_target_pairs={{0,64},{1,65},{2,66},{3,67},{4,68},{5,69},{6,70},{7,71},{8,72},{9,... | collective-permute-start | bytes 98312 | tf_op jit(solution)/shard_map/ppermute | solution.py:17
  76.2 16.8 %collective-permute-done.6 = f32[1,8,8,128]{3,2,1,0:T(8,128)S(1)} collective-permute-done((f32[1,8,8,128]{3,2,1,0:T(8,128)S(1)}, f32[1,8,8,128]{3,2,1,0:T(8,128)S(1)}, u32[]{:S(2)}, u32[]{:S(2)}) %collective-permute-start.6) | collective-permute-done | bytes 32800 | tf_op jit(solution)/shard_map/ppermute | solution.py:18
  93.0 9.6 %multiply_add_fusion.4 = f32[128,8,8,128]{3,2,1,0:T(8,128)S(1)} fusion(f32[128,8,8,128]{3,2,1,0:T(8,128)S(1)} %multiply_add_fusion.5, f32[128,8,8,128]{3,2,1,0:T(8,128)S(1)} %copy-done, f32[128,8,1,128]{3,2,1,0:T(1,128)S(1)} %bitcast.31, f32[130,1,8,128]{3,2,1,0:T(8,128)S(1)} %pad.78, f32[1,8,8,128]{3,2,1,0:T(8,128)S(1)} %collective-permute-done.6, ...), kind=kLoop, calls=%fused_computation.120 | loop fusion | flops 44040192 | bytes 23150592 | tf_op jit(solution)/shard_map/add | solution.py:69
  102.7 1.3 collective-permute-start.14
  104.6 3.1 %collective-permute-start.15 = (f32[128,1,8,128]{3,2,1,0:T(8,128)S(1)}, f32[128,1,8,128]{3,2,1,0:T(8,128)S(1)}, u32[]{:S(2)}, u32[]{:S(2)}) collective-permute-start(f32[128,1,8,128]{3,2,1,0:T(8,128)S(1)} %get-tuple-element.29), channel_id=1, source_target_pairs={{0,8},{8,16},{16,24},{24,32},{32,40},{40,48},{48,56},{1,9},{9,17},... | collective-permute-start | bytes 1572872 | tf_op jit(solution)/shard_map/ppermute | solution.py:17
  107.7 1.9 collective-permute-start.16
  109.6 4.0 %collective-permute-start.17 = (f32[128,8,1,128]{3,1,2,0:T(8,128)S(1)}, f32[128,8,1,128]{3,1,2,0:T(8,128)S(1)}, u32[]{:S(2)}, u32[]{:S(2)}) collective-permute-start(f32[128,8,1,128]{3,1,2,0:T(8,128)S(1)} %bitcast.42), channel_id=1, source_target_pairs={{0,1},{1,2},{2,3},{3,4},{4,5},{5,6},{6,7},{8,9},{9,10},{10,11},{11... | collective-permute-start | bytes 1572872 | tf_op jit(solution)/shard_map/ppermute | solution.py:17
  113.6 1.3 collective-permute-start.12
  114.9 6.0 %collective-permute-start.13 = (f32[1,8,8,128]{3,2,1,0:T(8,128)S(1)}, f32[1,8,8,128]{3,2,1,0:T(8,128)S(1)}, u32[]{:S(2)}, u32[]{:S(2)}) collective-permute-start(f32[1,8,8,128]{3,2,1,0:T(8,128)S(1)} %get-tuple-element.31), channel_id=1, source_target_pairs={{0,64},{1,65},{2,66},{3,67},{4,68},{5,69},{6,70},{7,71},{8,72},{9,... | collective-permute-start | bytes 98312 | tf_op jit(solution)/shard_map/ppermute | solution.py:17
  121.1 14.8 %collective-permute-done.12 = f32[1,8,8,128]{3,2,1,0:T(8,128)S(1)} collective-permute-done((f32[1,8,8,128]{3,2,1,0:T(8,128)S(1)}, f32[1,8,8,128]{3,2,1,0:T(8,128)S(1)}, u32[]{:S(2)}, u32[]{:S(2)}) %collective-permute-start.12) | collective-permute-done | bytes 32800 | tf_op jit(solution)/shard_map/ppermute | solution.py:18
  135.9 9.6 %multiply_add_fusion.3 = f32[128,8,8,128]{3,2,1,0:T(8,128)S(1)} fusion(f32[128,8,8,128]{3,2,1,0:T(8,128)S(1)} %multiply_add_fusion.4, f32[128,8,8,128]{3,2,1,0:T(8,128)S(1)} %copy-done, f32[128,8,1,128]{3,2,1,0:T(1,128)S(1)} %bitcast.32, f32[130,1,8,128]{3,2,1,0:T(8,128)S(1)} %pad.82, f32[1,8,8,128]{3,2,1,0:T(8,128)S(1)} %collective-permute-done.12, ...), kind=kLoop, calls=%fused_computation.119 | loop fusion | flops 44040192 | bytes 23150592 | tf_op jit(solution)/shard_map/add | solution.py:69
  145.6 1.3 collective-permute-start.20
  147.6 3.1 %collective-permute-start.21 = (f32[128,1,8,128]{3,2,1,0:T(8,128)S(1)}, f32[128,1,8,128]{3,2,1,0:T(8,128)S(1)}, u32[]{:S(2)}, u32[]{:S(2)}) collective-permute-start(f32[128,1,8,128]{3,2,1,0:T(8,128)S(1)} %get-tuple-element.23), channel_id=1, source_target_pairs={{0,8},{8,16},{16,24},{24,32},{32,40},{40,48},{48,56},{1,9},{9,17},... | collective-permute-start | bytes 1572872 | tf_op jit(solution)/shard_map/ppermute | solution.py:17
  150.7 1.9 collective-permute-start.23
  152.6 4.8 %collective-permute-start.22 = (f32[128,8,1,128]{3,1,2,0:T(8,128)S(1)}, f32[128,8,1,128]{3,1,2,0:T(8,128)S(1)}, u32[]{:S(2)}, u32[]{:S(2)}) collective-permute-start(f32[128,8,1,128]{3,1,2,0:T(8,128)S(1)} %bitcast.43), channel_id=1, source_target_pairs={{1,0},{2,1},{3,2},{4,3},{5,4},{6,5},{7,6},{9,8},{10,9},{11,10},{12... | collective-permute-start | bytes 1572872 | tf_op jit(solution)/shard_map/ppermute | solution.py:18
  158.7 6.2 %collective-permute-start.19 = (f32[1,8,8,128]{3,2,1,0:T(8,128)S(1)}, f32[1,8,8,128]{3,2,1,0:T(8,128)S(1)}, u32[]{:S(2)}, u32[]{:S(2)}) collective-permute-start(f32[1,8,8,128]{3,2,1,0:T(8,128)S(1)} %get-tuple-element.25), channel_id=1, source_target_pairs={{0,64},{1,65},{2,66},{3,67},{4,68},{5,69},{6,70},{7,71},{8,72},{9,... | collective-permute-start | bytes 98312 | tf_op jit(solution)/shard_map/ppermute | solution.py:17
  165.1 12.6 %collective-permute-done.18 = f32[1,8,8,128]{3,2,1,0:T(8,128)S(1)} collective-permute-done((f32[1,8,8,128]{3,2,1,0:T(8,128)S(1)}, f32[1,8,8,128]{3,2,1,0:T(8,128)S(1)}, u32[]{:S(2)}, u32[]{:S(2)}) %collective-permute-start.18) | collective-permute-done | bytes 32800 | tf_op jit(solution)/shard_map/ppermute | solution.py:18
  177.7 9.6 %multiply_add_fusion.2 = f32[128,8,8,128]{3,2,1,0:T(8,128)S(1)} fusion(f32[128,8,8,128]{3,2,1,0:T(8,128)S(1)} %multiply_add_fusion.3, f32[128,8,8,128]{3,2,1,0:T(8,128)S(1)} %copy-done, f32[128,8,1,128]{3,2,1,0:T(1,128)S(1)} %bitcast.38, f32[130,1,8,128]{3,2,1,0:T(8,128)S(1)} %pad.86, f32[1,8,8,128]{3,2,1,0:T(8,128)S(1)} %collective-permute-done.18, ...), kind=kLoop, calls=%fused_computation.118 | loop fusion | flops 44040192 | bytes 23150592 | tf_op jit(solution)/shard_map/add | solution.py:69
  189.3 3.3 %collective-permute-start.27 = (f32[128,1,8,128]{3,2,1,0:T(8,128)S(1)}, f32[128,1,8,128]{3,2,1,0:T(8,128)S(1)}, u32[]{:S(2)}, u32[]{:S(2)}) collective-permute-start(f32[128,1,8,128]{3,2,1,0:T(8,128)S(1)} %get-tuple-element.17), channel_id=1, source_target_pairs={{0,8},{8,16},{16,24},{24,32},{32,40},{40,48},{48,56},{1,9},{9,17},... | collective-permute-start | bytes 1572872 | tf_op jit(solution)/shard_map/ppermute | solution.py:17
  192.7 4.2 %collective-permute-start.28 = (f32[128,8,1,128]{3,1,2,0:T(8,128)S(1)}, f32[128,8,1,128]{3,1,2,0:T(8,128)S(1)}, u32[]{:S(2)}, u32[]{:S(2)}) collective-permute-start(f32[128,8,1,128]{3,1,2,0:T(8,128)S(1)} %bitcast.50), channel_id=1, source_target_pairs={{1,0},{2,1},{3,2},{4,3},{5,4},{6,5},{7,6},{9,8},{10,9},{11,10},{12... | collective-permute-start | bytes 1572872 | tf_op jit(solution)/shard_map/ppermute | solution.py:18
  196.8 1.9 collective-permute-start.29
  200.1 6.0 %collective-permute-start.25 = (f32[1,8,8,128]{3,2,1,0:T(8,128)S(1)}, f32[1,8,8,128]{3,2,1,0:T(8,128)S(1)}, u32[]{:S(2)}, u32[]{:S(2)}) collective-permute-start(f32[1,8,8,128]{3,2,1,0:T(8,128)S(1)} %get-tuple-element.19), channel_id=1, source_target_pairs={{0,64},{1,65},{2,66},{3,67},{4,68},{5,69},{6,70},{7,71},{8,72},{9,... | collective-permute-start | bytes 98312 | tf_op jit(solution)/shard_map/ppermute | solution.py:17
  206.3 18.5 %collective-permute-done.24 = f32[1,8,8,128]{3,2,1,0:T(8,128)S(1)} collective-permute-done((f32[1,8,8,128]{3,2,1,0:T(8,128)S(1)}, f32[1,8,8,128]{3,2,1,0:T(8,128)S(1)}, u32[]{:S(2)}, u32[]{:S(2)}) %collective-permute-start.24) | collective-permute-done | bytes 32800 | tf_op jit(solution)/shard_map/ppermute | solution.py:18
  224.8 9.6 %multiply_add_fusion.1 = f32[128,8,8,128]{3,2,1,0:T(8,128)S(1)} fusion(f32[128,8,8,128]{3,2,1,0:T(8,128)S(1)} %multiply_add_fusion.2, f32[128,8,8,128]{3,2,1,0:T(8,128)S(1)} %copy-done, f32[128,8,1,128]{3,2,1,0:T(1,128)S(1)} %bitcast.34, f32[130,1,8,128]{3,2,1,0:T(8,128)S(1)} %pad.90, f32[1,8,8,128]{3,2,1,0:T(8,128)S(1)} %collective-permute-done.24, ...), kind=kLoop, calls=%fused_computation.117 | loop fusion | flops 44040192 | bytes 23150592 | tf_op jit(solution)/shard_map/add | solution.py:69
  234.5 1.3 collective-permute-start.32
  236.4 3.1 %collective-permute-start.33 = (f32[128,1,8,128]{3,2,1,0:T(8,128)S(1)}, f32[128,1,8,128]{3,2,1,0:T(8,128)S(1)}, u32[]{:S(2)}, u32[]{:S(2)}) collective-permute-start(f32[128,1,8,128]{3,2,1,0:T(8,128)S(1)} %get-tuple-element.11), channel_id=1, source_target_pairs={{0,8},{8,16},{16,24},{24,32},{32,40},{40,48},{48,56},{1,9},{9,17},... | collective-permute-start | bytes 1572872 | tf_op jit(solution)/shard_map/ppermute | solution.py:17
  239.5 1.9 collective-permute-start.34
  241.4 4.0 %collective-permute-start.35 = (f32[128,8,1,128]{3,1,2,0:T(8,128)S(1)}, f32[128,8,1,128]{3,1,2,0:T(8,128)S(1)}, u32[]{:S(2)}, u32[]{:S(2)}) collective-permute-start(f32[128,8,1,128]{3,1,2,0:T(8,128)S(1)} %bitcast.45), channel_id=1, source_target_pairs={{0,1},{1,2},{2,3},{3,4},{4,5},{5,6},{6,7},{8,9},{9,10},{10,11},{11... | collective-permute-start | bytes 1572872 | tf_op jit(solution)/shard_map/ppermute | solution.py:17
  246.7 6.0 %collective-permute-start.31 = (f32[1,8,8,128]{3,2,1,0:T(8,128)S(1)}, f32[1,8,8,128]{3,2,1,0:T(8,128)S(1)}, u32[]{:S(2)}, u32[]{:S(2)}) collective-permute-start(f32[1,8,8,128]{3,2,1,0:T(8,128)S(1)} %get-tuple-element.13), channel_id=1, source_target_pairs={{0,64},{1,65},{2,66},{3,67},{4,68},{5,69},{6,70},{7,71},{8,72},{9,... | collective-permute-start | bytes 98312 | tf_op jit(solution)/shard_map/ppermute | solution.py:17
  252.9 15.5 %collective-permute-done.30 = f32[1,8,8,128]{3,2,1,0:T(8,128)S(1)} collective-permute-done((f32[1,8,8,128]{3,2,1,0:T(8,128)S(1)}, f32[1,8,8,128]{3,2,1,0:T(8,128)S(1)}, u32[]{:S(2)}, u32[]{:S(2)}) %collective-permute-start.30) | collective-permute-done | bytes 32800 | tf_op jit(solution)/shard_map/ppermute | solution.py:18
  268.4 11.1 %add_reduce_fusion = (f32[8,8,128]{2,1,0:T(8,128)S(1)}, f32[8,8,128]{2,1,0:T(8,128)S(1)}, f32[128,8,8,128]{3,2,1,0:T(8,128)}) fusion(f32[128,8,8,128]{3,2,1,0:T(8,128)S(1)} %multiply_add_fusion.1, f32[128,8,8,128]{3,2,1,0:T(8,128)S(1)} %copy-done, f32[130,1,8,128]{3,2,1,0:T(8,128)S(1)} %pad.94, f32[1,8,8,128]{3,2,1,0:T(8,128)S(1)} %collective-permute-done.30, ...), kind=kLoop, calls=%fused_computation.122 | loop fusion | flops 48218112 | bytes 23216128 | tf_op jit(solution)/shard_map/reduce_sum | solution.py:81
  279.6 8.4 %all_to_all.6 = f32[2,1,16384]{2,1,0:T(1,128)S(1)} all-to-all(f32[2,1,16384]{2,1,0:T(1,128)S(1)} %broadcast_in_dim.2), channel_id=1, replica_groups=mesh['south'=2,'east'=8,'down'=8] {'south'}, dimensions={0} | all-to-all | bytes 262144 | tf_op jit(solution)/shard_map/all_to_all | solution.py:31
  288.3 5.1 %subtract_multiply_fusion = f32[128,8,8,128]{3,2,1,0:T(8,128)} fusion(f32[128,8,8,128]{3,2,1,0:T(8,128)} %get-tuple-element.8, f32[8,8,128]{2,1,0:T(8,128)S(1)} %get-tuple-element.46, f32[8,8,128]{2,1,0:T(8,128)S(1)} %get-tuple-element.45), kind=kLoop, calls=%fused_computation.114 | loop fusion | flops 2097152 | bytes 8454144 | tf_op jit(solution)/shard_map/mul | solution.py:87
  (75 shorter events, 13.1 us)
Async XLA Ops:
  1.9 43.7 %collective-permute-start.2 = (f32[128,1,8,128]{3,2,1,0:T(8,128)S(1)}, f32[128,1,8,128]{3,2,1,0:T(8,128)S(1)}, u32[]{:S(2)}, u32[]{:S(2)}) collective-permute-start(f32[128,1,8,128]{3,2,1,0:T(8,128)S(1)} %get-tuple-element.42), channel_id=1, source_target_pairs={{8,0},{16,8},{24,16},{32,24},{40,32},{48,40},{56,48},{9,1},{17,9},... | collective-permute-start | bytes 1572872 | tf_op jit(solution)/shard_map/ppermute | solution.py:18
  3.2 42.5 %collective-permute-start.3 = (f32[128,1,8,128]{3,2,1,0:T(8,128)S(1)}, f32[128,1,8,128]{3,2,1,0:T(8,128)S(1)}, u32[]{:S(2)}, u32[]{:S(2)}) collective-permute-start(f32[128,1,8,128]{3,2,1,0:T(8,128)S(1)} %get-tuple-element.41), channel_id=1, source_target_pairs={{0,8},{8,16},{16,24},{24,32},{32,40},{40,48},{48,56},{1,9},{9,17},... | collective-permute-start | bytes 1572872 | tf_op jit(solution)/shard_map/ppermute | solution.py:17
  6.3 39.5 %copy-start.2 = (f32[128,8,8,128]{3,2,1,0:T(8,128)S(1)}, f32[128,8,8,128]{3,2,1,0:T(8,128)}, u32[]{:S(2)}) copy-start(f32[128,8,8,128]{3,2,1,0:T(8,128)} %param.5) | copy-start | bytes 12582916
  11.0 34.7 %collective-permute-start.4 = (f32[128,8,1,128]{3,1,2,0:T(8,128)S(1)}, f32[128,8,1,128]{3,1,2,0:T(8,128)}, u32[]{:S(2)}, u32[]{:S(2)}) collective-permute-start(f32[128,8,1,128]{3,1,2,0:T(8,128)S(1)} %bitcast.46), channel_id=1, source_target_pairs={{1,0},{2,1},{3,2},{4,3},{5,4},{6,5},{7,6},{9,8},{10,9},{11,10},{12... | collective-permute-start | bytes 1572872 | tf_op jit(solution)/shard_map/ppermute | solution.py:18
  14.3 31.5 %collective-permute-start.5 = (f32[128,8,1,128]{3,1,2,0:T(8,128)S(1)}, f32[128,8,1,128]{3,1,2,0:T(8,128)}, u32[]{:S(2)}, u32[]{:S(2)}) collective-permute-start(f32[128,8,1,128]{3,1,2,0:T(8,128)S(1)} %bitcast.40), channel_id=1, source_target_pairs={{0,1},{1,2},{2,3},{3,4},{4,5},{5,6},{6,7},{8,9},{9,10},{10,11},{11... | collective-permute-start | bytes 1572872 | tf_op jit(solution)/shard_map/ppermute | solution.py:17
  18.5 19.9 %collective-permute-start.1 = (f32[1,8,8,128]{3,2,1,0:T(8,128)S(1)}, f32[1,8,8,128]{3,2,1,0:T(8,128)S(1)}, u32[]{:S(2)}, u32[]{:S(2)}) collective-permute-start(f32[1,8,8,128]{3,2,1,0:T(8,128)S(1)} %get-tuple-element.44), channel_id=1, source_target_pairs={{0,64},{1,65},{2,66},{3,67},{4,68},{5,69},{6,70},{7,71},{8,72},{9,... | collective-permute-start | bytes 98312 | tf_op jit(solution)/shard_map/ppermute | solution.py:17
  38.3 7.3 %collective-permute-start = (f32[1,8,8,128]{3,2,1,0:T(8,128)S(1)}, f32[1,8,8,128]{3,2,1,0:T(8,128)S(1)}, u32[]{:S(2)}, u32[]{:S(2)}) collective-permute-start(f32[1,8,8,128]{3,2,1,0:T(8,128)S(1)} %get-tuple-element.43), channel_id=1, source_target_pairs={{64,0},{65,1},{66,2},{67,3},{68,4},{69,5},{70,6},{71,7},{72,8},{73... | collective-permute-start | bytes 98312 | tf_op jit(solution)/shard_map/ppermute | solution.py:18
  39.6 6.1 %copy-start = (f32[128,8,8,128]{3,2,1,0:T(8,128)S(1)}, f32[128,8,8,128]{3,2,1,0:T(8,128)}, u32[]{:S(2)}) copy-start(f32[128,8,8,128]{3,2,1,0:T(8,128)} %param.7) | copy-start | bytes 12582916
  39.6 6.1 %copy-start.1 = (f32[128,8,8,128]{3,2,1,0:T(8,128)S(1)}, f32[128,8,8,128]{3,2,1,0:T(8,128)}, u32[]{:S(2)}) copy-start(f32[128,8,8,128]{3,2,1,0:T(8,128)} %param.6) | copy-start | bytes 12582916
  57.7 12.2 %collective-permute-start.8 = (f32[128,1,8,128]{3,2,1,0:T(8,128)S(1)}, f32[128,1,8,128]{3,2,1,0:T(8,128)S(1)}, u32[]{:S(2)}, u32[]{:S(2)}) collective-permute-start(f32[128,1,8,128]{3,2,1,0:T(8,128)S(1)} %get-tuple-element.36), channel_id=1, source_target_pairs={{8,0},{16,8},{24,16},{32,24},{40,32},{48,40},{56,48},{9,1},{17,9},... | collective-permute-start | bytes 1572872 | tf_op jit(solution)/shard_map/ppermute | solution.py:18
  59.7 16.4 %collective-permute-start.9 = (f32[128,1,8,128]{3,2,1,0:T(8,128)S(1)}, f32[128,1,8,128]{3,2,1,0:T(8,128)S(1)}, u32[]{:S(2)}, u32[]{:S(2)}) collective-permute-start(f32[128,1,8,128]{3,2,1,0:T(8,128)S(1)} %get-tuple-element.35), channel_id=1, source_target_pairs={{0,8},{8,16},{16,24},{24,32},{32,40},{40,48},{48,56},{1,9},{9,17},... | collective-permute-start | bytes 1572872 | tf_op jit(solution)/shard_map/ppermute | solution.py:17
  62.8 30.2 %collective-permute-start.10 = (f32[128,8,1,128]{3,1,2,0:T(8,128)S(1)}, f32[128,8,1,128]{3,1,2,0:T(8,128)S(1)}, u32[]{:S(2)}, u32[]{:S(2)}) collective-permute-start(f32[128,8,1,128]{3,1,2,0:T(8,128)S(1)} %bitcast.47), channel_id=1, source_target_pairs={{1,0},{2,1},{3,2},{4,3},{5,4},{6,5},{7,6},{9,8},{10,9},{11,10},{12... | collective-permute-start | bytes 1572872 | tf_op jit(solution)/shard_map/ppermute | solution.py:18
  65.2 27.7 %collective-permute-start.11 = (f32[128,8,1,128]{3,1,2,0:T(8,128)S(1)}, f32[128,8,1,128]{3,1,2,0:T(8,128)S(1)}, u32[]{:S(2)}, u32[]{:S(2)}) collective-permute-start(f32[128,8,1,128]{3,1,2,0:T(8,128)S(1)} %bitcast.41), channel_id=1, source_target_pairs={{0,1},{1,2},{2,3},{3,4},{4,5},{5,6},{6,7},{8,9},{9,10},{10,11},{11... | collective-permute-start | bytes 1572872 | tf_op jit(solution)/shard_map/ppermute | solution.py:17
  68.7 24.3 %collective-permute-start.6 = (f32[1,8,8,128]{3,2,1,0:T(8,128)S(1)}, f32[1,8,8,128]{3,2,1,0:T(8,128)S(1)}, u32[]{:S(2)}, u32[]{:S(2)}) collective-permute-start(f32[1,8,8,128]{3,2,1,0:T(8,128)S(1)} %get-tuple-element.38), channel_id=1, source_target_pairs={{64,0},{65,1},{66,2},{67,3},{68,4},{69,5},{70,6},{71,7},{72,8},{73... | collective-permute-start | bytes 98312 | tf_op jit(solution)/shard_map/ppermute | solution.py:18
  70.0 23.0 %collective-permute-start.7 = (f32[1,8,8,128]{3,2,1,0:T(8,128)S(1)}, f32[1,8,8,128]{3,2,1,0:T(8,128)S(1)}, u32[]{:S(2)}, u32[]{:S(2)}) collective-permute-start(f32[1,8,8,128]{3,2,1,0:T(8,128)S(1)} %get-tuple-element.37), channel_id=1, source_target_pairs={{0,64},{1,65},{2,66},{3,67},{4,68},{5,69},{6,70},{7,71},{8,72},{9,... | collective-permute-start | bytes 98312 | tf_op jit(solution)/shard_map/ppermute | solution.py:17
  102.7 12.2 %collective-permute-start.14 = (f32[128,1,8,128]{3,2,1,0:T(8,128)S(1)}, f32[128,1,8,128]{3,2,1,0:T(8,128)S(1)}, u32[]{:S(2)}, u32[]{:S(2)}) collective-permute-start(f32[128,1,8,128]{3,2,1,0:T(8,128)S(1)} %get-tuple-element.30), channel_id=1, source_target_pairs={{8,0},{16,8},{24,16},{32,24},{40,32},{48,40},{56,48},{9,1},{17,9},... | collective-permute-start | bytes 1572872 | tf_op jit(solution)/shard_map/ppermute | solution.py:18
  104.6 16.4 %collective-permute-start.15 = (f32[128,1,8,128]{3,2,1,0:T(8,128)S(1)}, f32[128,1,8,128]{3,2,1,0:T(8,128)S(1)}, u32[]{:S(2)}, u32[]{:S(2)}) collective-permute-start(f32[128,1,8,128]{3,2,1,0:T(8,128)S(1)} %get-tuple-element.29), channel_id=1, source_target_pairs={{0,8},{8,16},{16,24},{24,32},{32,40},{40,48},{48,56},{1,9},{9,17},... | collective-permute-start | bytes 1572872 | tf_op jit(solution)/shard_map/ppermute | solution.py:17
  107.7 28.2 %collective-permute-start.16 = (f32[128,8,1,128]{3,1,2,0:T(8,128)S(1)}, f32[128,8,1,128]{3,1,2,0:T(8,128)S(1)}, u32[]{:S(2)}, u32[]{:S(2)}) collective-permute-start(f32[128,8,1,128]{3,1,2,0:T(8,128)S(1)} %bitcast.48), channel_id=1, source_target_pairs={{1,0},{2,1},{3,2},{4,3},{5,4},{6,5},{7,6},{9,8},{10,9},{11,10},{12... | collective-permute-start | bytes 1572872 | tf_op jit(solution)/shard_map/ppermute | solution.py:18
  109.6 26.3 %collective-permute-start.17 = (f32[128,8,1,128]{3,1,2,0:T(8,128)S(1)}, f32[128,8,1,128]{3,1,2,0:T(8,128)S(1)}, u32[]{:S(2)}, u32[]{:S(2)}) collective-permute-start(f32[128,8,1,128]{3,1,2,0:T(8,128)S(1)} %bitcast.42), channel_id=1, source_target_pairs={{0,1},{1,2},{2,3},{3,4},{4,5},{5,6},{6,7},{8,9},{9,10},{10,11},{11... | collective-permute-start | bytes 1572872 | tf_op jit(solution)/shard_map/ppermute | solution.py:17
  113.6 22.3 %collective-permute-start.12 = (f32[1,8,8,128]{3,2,1,0:T(8,128)S(1)}, f32[1,8,8,128]{3,2,1,0:T(8,128)S(1)}, u32[]{:S(2)}, u32[]{:S(2)}) collective-permute-start(f32[1,8,8,128]{3,2,1,0:T(8,128)S(1)} %get-tuple-element.32), channel_id=1, source_target_pairs={{64,0},{65,1},{66,2},{67,3},{68,4},{69,5},{70,6},{71,7},{72,8},{73... | collective-permute-start | bytes 98312 | tf_op jit(solution)/shard_map/ppermute | solution.py:18
  114.9 21.0 %collective-permute-start.13 = (f32[1,8,8,128]{3,2,1,0:T(8,128)S(1)}, f32[1,8,8,128]{3,2,1,0:T(8,128)S(1)}, u32[]{:S(2)}, u32[]{:S(2)}) collective-permute-start(f32[1,8,8,128]{3,2,1,0:T(8,128)S(1)} %get-tuple-element.31), channel_id=1, source_target_pairs={{0,64},{1,65},{2,66},{3,67},{4,68},{5,69},{6,70},{7,71},{8,72},{9,... | collective-permute-start | bytes 98312 | tf_op jit(solution)/shard_map/ppermute | solution.py:17
  145.6 13.1 %collective-permute-start.20 = (f32[128,1,8,128]{3,2,1,0:T(8,128)S(1)}, f32[128,1,8,128]{3,2,1,0:T(8,128)S(1)}, u32[]{:S(2)}, u32[]{:S(2)}) collective-permute-start(f32[128,1,8,128]{3,2,1,0:T(8,128)S(1)} %get-tuple-element.24), channel_id=1, source_target_pairs={{8,0},{16,8},{24,16},{32,24},{40,32},{48,40},{56,48},{9,1},{17,9},... | collective-permute-start | bytes 1572872 | tf_op jit(solution)/shard_map/ppermute | solution.py:18
  147.6 17.4 %collective-permute-start.21 = (f32[128,1,8,128]{3,2,1,0:T(8,128)S(1)}, f32[128,1,8,128]{3,2,1,0:T(8,128)S(1)}, u32[]{:S(2)}, u32[]{:S(2)}) collective-permute-start(f32[128,1,8,128]{3,2,1,0:T(8,128)S(1)} %get-tuple-element.23), channel_id=1, source_target_pairs={{0,8},{8,16},{16,24},{24,32},{32,40},{40,48},{48,56},{1,9},{9,17},... | collective-permute-start | bytes 1572872 | tf_op jit(solution)/shard_map/ppermute | solution.py:17
  150.7 27.0 %collective-permute-start.23 = (f32[128,8,1,128]{3,1,2,0:T(8,128)S(1)}, f32[128,8,1,128]{3,1,2,0:T(8,128)S(1)}, u32[]{:S(2)}, u32[]{:S(2)}) collective-permute-start(f32[128,8,1,128]{3,1,2,0:T(8,128)S(1)} %bitcast.49), channel_id=1, source_target_pairs={{0,1},{1,2},{2,3},{3,4},{4,5},{5,6},{6,7},{8,9},{9,10},{10,11},{11... | collective-permute-start | bytes 1572872 | tf_op jit(solution)/shard_map/ppermute | solution.py:17
  152.6 25.1 %collective-permute-start.22 = (f32[128,8,1,128]{3,1,2,0:T(8,128)S(1)}, f32[128,8,1,128]{3,1,2,0:T(8,128)S(1)}, u32[]{:S(2)}, u32[]{:S(2)}) collective-permute-start(f32[128,8,1,128]{3,1,2,0:T(8,128)S(1)} %bitcast.43), channel_id=1, source_target_pairs={{1,0},{2,1},{3,2},{4,3},{5,4},{6,5},{7,6},{9,8},{10,9},{11,10},{12... | collective-permute-start | bytes 1572872 | tf_op jit(solution)/shard_map/ppermute | solution.py:18
  157.4 20.2 %collective-permute-start.18 = (f32[1,8,8,128]{3,2,1,0:T(8,128)S(1)}, f32[1,8,8,128]{3,2,1,0:T(8,128)S(1)}, u32[]{:S(2)}, u32[]{:S(2)}) collective-permute-start(f32[1,8,8,128]{3,2,1,0:T(8,128)S(1)} %get-tuple-element.26), channel_id=1, source_target_pairs={{64,0},{65,1},{66,2},{67,3},{68,4},{69,5},{70,6},{71,7},{72,8},{73... | collective-permute-start | bytes 98312 | tf_op jit(solution)/shard_map/ppermute | solution.py:18
  158.7 18.9 %collective-permute-start.19 = (f32[1,8,8,128]{3,2,1,0:T(8,128)S(1)}, f32[1,8,8,128]{3,2,1,0:T(8,128)S(1)}, u32[]{:S(2)}, u32[]{:S(2)}) collective-permute-start(f32[1,8,8,128]{3,2,1,0:T(8,128)S(1)} %get-tuple-element.25), channel_id=1, source_target_pairs={{0,64},{1,65},{2,66},{3,67},{4,68},{5,69},{6,70},{7,71},{8,72},{9,... | collective-permute-start | bytes 98312 | tf_op jit(solution)/shard_map/ppermute | solution.py:17
  187.4 12.7 %collective-permute-start.26 = (f32[128,1,8,128]{3,2,1,0:T(8,128)S(1)}, f32[128,1,8,128]{3,2,1,0:T(8,128)S(1)}, u32[]{:S(2)}, u32[]{:S(2)}) collective-permute-start(f32[128,1,8,128]{3,2,1,0:T(8,128)S(1)} %get-tuple-element.18), channel_id=1, source_target_pairs={{8,0},{16,8},{24,16},{32,24},{40,32},{48,40},{56,48},{9,1},{17,9},... | collective-permute-start | bytes 1572872 | tf_op jit(solution)/shard_map/ppermute | solution.py:18
  189.3 16.9 %collective-permute-start.27 = (f32[128,1,8,128]{3,2,1,0:T(8,128)S(1)}, f32[128,1,8,128]{3,2,1,0:T(8,128)S(1)}, u32[]{:S(2)}, u32[]{:S(2)}) collective-permute-start(f32[128,1,8,128]{3,2,1,0:T(8,128)S(1)} %get-tuple-element.17), channel_id=1, source_target_pairs={{0,8},{8,16},{16,24},{24,32},{32,40},{40,48},{48,56},{1,9},{9,17},... | collective-permute-start | bytes 1572872 | tf_op jit(solution)/shard_map/ppermute | solution.py:17
  192.7 32.1 %collective-permute-start.28 = (f32[128,8,1,128]{3,1,2,0:T(8,128)S(1)}, f32[128,8,1,128]{3,1,2,0:T(8,128)S(1)}, u32[]{:S(2)}, u32[]{:S(2)}) collective-permute-start(f32[128,8,1,128]{3,1,2,0:T(8,128)S(1)} %bitcast.50), channel_id=1, source_target_pairs={{1,0},{2,1},{3,2},{4,3},{5,4},{6,5},{7,6},{9,8},{10,9},{11,10},{12... | collective-permute-start | bytes 1572872 | tf_op jit(solution)/shard_map/ppermute | solution.py:18
  196.8 27.9 %collective-permute-start.29 = (f32[128,8,1,128]{3,1,2,0:T(8,128)S(1)}, f32[128,8,1,128]{3,1,2,0:T(8,128)S(1)}, u32[]{:S(2)}, u32[]{:S(2)}) collective-permute-start(f32[128,8,1,128]{3,1,2,0:T(8,128)S(1)} %bitcast.44), channel_id=1, source_target_pairs={{0,1},{1,2},{2,3},{3,4},{4,5},{5,6},{6,7},{8,9},{9,10},{10,11},{11... | collective-permute-start | bytes 1572872 | tf_op jit(solution)/shard_map/ppermute | solution.py:17
  198.8 26.0 %collective-permute-start.24 = (f32[1,8,8,128]{3,2,1,0:T(8,128)S(1)}, f32[1,8,8,128]{3,2,1,0:T(8,128)S(1)}, u32[]{:S(2)}, u32[]{:S(2)}) collective-permute-start(f32[1,8,8,128]{3,2,1,0:T(8,128)S(1)} %get-tuple-element.20), channel_id=1, source_target_pairs={{64,0},{65,1},{66,2},{67,3},{68,4},{69,5},{70,6},{71,7},{72,8},{73... | collective-permute-start | bytes 98312 | tf_op jit(solution)/shard_map/ppermute | solution.py:18
  200.1 24.7 %collective-permute-start.25 = (f32[1,8,8,128]{3,2,1,0:T(8,128)S(1)}, f32[1,8,8,128]{3,2,1,0:T(8,128)S(1)}, u32[]{:S(2)}, u32[]{:S(2)}) collective-permute-start(f32[1,8,8,128]{3,2,1,0:T(8,128)S(1)} %get-tuple-element.19), channel_id=1, source_target_pairs={{0,64},{1,65},{2,66},{3,67},{4,68},{5,69},{6,70},{7,71},{8,72},{9,... | collective-permute-start | bytes 98312 | tf_op jit(solution)/shard_map/ppermute | solution.py:17
  234.5 12.2 %collective-permute-start.32 = (f32[128,1,8,128]{3,2,1,0:T(8,128)S(1)}, f32[128,1,8,128]{3,2,1,0:T(8,128)S(1)}, u32[]{:S(2)}, u32[]{:S(2)}) collective-permute-start(f32[128,1,8,128]{3,2,1,0:T(8,128)S(1)} %get-tuple-element.12), channel_id=1, source_target_pairs={{8,0},{16,8},{24,16},{32,24},{40,32},{48,40},{56,48},{9,1},{17,9},... | collective-permute-start | bytes 1572872 | tf_op jit(solution)/shard_map/ppermute | solution.py:18
  236.4 16.4 %collective-permute-start.33 = (f32[128,1,8,128]{3,2,1,0:T(8,128)S(1)}, f32[128,1,8,128]{3,2,1,0:T(8,128)S(1)}, u32[]{:S(2)}, u32[]{:S(2)}) collective-permute-start(f32[128,1,8,128]{3,2,1,0:T(8,128)S(1)} %get-tuple-element.11), channel_id=1, source_target_pairs={{0,8},{8,16},{16,24},{24,32},{32,40},{40,48},{48,56},{1,9},{9,17},... | collective-permute-start | bytes 1572872 | tf_op jit(solution)/shard_map/ppermute | solution.py:17
  239.5 28.9 %collective-permute-start.34 = (f32[128,8,1,128]{3,1,2,0:T(8,128)S(1)}, f32[128,8,1,128]{3,1,2,0:T(8,128)S(1)}, u32[]{:S(2)}, u32[]{:S(2)}) collective-permute-start(f32[128,8,1,128]{3,1,2,0:T(8,128)S(1)} %bitcast.51), channel_id=1, source_target_pairs={{1,0},{2,1},{3,2},{4,3},{5,4},{6,5},{7,6},{9,8},{10,9},{11,10},{12... | collective-permute-start | bytes 1572872 | tf_op jit(solution)/shard_map/ppermute | solution.py:18
  241.4 26.9 %collective-permute-start.35 = (f32[128,8,1,128]{3,1,2,0:T(8,128)S(1)}, f32[128,8,1,128]{3,1,2,0:T(8,128)S(1)}, u32[]{:S(2)}, u32[]{:S(2)}) collective-permute-start(f32[128,8,1,128]{3,1,2,0:T(8,128)S(1)} %bitcast.45), channel_id=1, source_target_pairs={{0,1},{1,2},{2,3},{3,4},{4,5},{5,6},{6,7},{8,9},{9,10},{10,11},{11... | collective-permute-start | bytes 1572872 | tf_op jit(solution)/shard_map/ppermute | solution.py:17
  245.4 23.0 %collective-permute-start.30 = (f32[1,8,8,128]{3,2,1,0:T(8,128)S(1)}, f32[1,8,8,128]{3,2,1,0:T(8,128)S(1)}, u32[]{:S(2)}, u32[]{:S(2)}) collective-permute-start(f32[1,8,8,128]{3,2,1,0:T(8,128)S(1)} %get-tuple-element.14), channel_id=1, source_target_pairs={{64,0},{65,1},{66,2},{67,3},{68,4},{69,5},{70,6},{71,7},{72,8},{73... | collective-permute-start | bytes 98312 | tf_op jit(solution)/shard_map/ppermute | solution.py:18
  246.7 21.7 %collective-permute-start.31 = (f32[1,8,8,128]{3,2,1,0:T(8,128)S(1)}, f32[1,8,8,128]{3,2,1,0:T(8,128)S(1)}, u32[]{:S(2)}, u32[]{:S(2)}) collective-permute-start(f32[1,8,8,128]{3,2,1,0:T(8,128)S(1)} %get-tuple-element.13), channel_id=1, source_target_pairs={{0,64},{1,65},{2,66},{3,67},{4,68},{5,69},{6,70},{7,71},{8,72},{9,... | collective-permute-start | bytes 98312 | tf_op jit(solution)/shard_map/ppermute | solution.py:17
where the time goes:
time: 295 us; the launch traced here: 293 us
  starting transfers between devices  107 us (36%)
  waiting for transfers between devices  96.5 us (33%)
  other arithmetic  66.7 us (23%)
  local copies, waits for them, and re-layouts  13.7 us (5%)
  blocking collectives  8.44 us (3%)
    ppermute x18, waiting for transfers between devices, with_halo(): lax.ppermute(leading, axis, [(b, a) for a, b in up])  81.6 us
    ppermute x18, starting transfers between devices, with_halo(): lax.ppermute(last, axis, up)  72.5 us
    add x5, other arithmetic, advance(): middle - flow_j * slopes[0] - flow_i * slopes[1] - flow_k * slopes[2]  50.3 us
    ppermute x18, starting transfers between devices, with_halo(): lax.ppermute(leading, axis, [(b, a) for a, b in up])  34 us
    ppermute x18, waiting for transfers between devices, with_halo(): lax.ppermute(last, axis, up)  15 us
    reduce_sum x1, other arithmetic, per_device(): jnp.sum(moved, axis=0, keepdims=True)  11.1 us
    slice x16, local copies, waits for them, and re-layouts, with_halo(): last = lax.slice_in_dim(shard, length - width, length, axis=dim)  9.09 us
    all_to_all x1, blocking collectives, sent_to_all(): lax.all_to_all(jnp.broadcast_to(shard[None], (devices, *shard.shape)), ax...  8.44 us
  transfers between devices with their start and end apart: 36, of which 7 were waited for; matrix products, arithmetic and copies ran while one was open for 4% of the time, Pallas kernels for 0%

commit v1 on v0

v1 whole, which is shorter than its diff:
```python
import functools

import jax
import jax.numpy as jnp
from jax import lax
from jax.experimental import pallas as pl
from jax.experimental.pallas import tpu as pltpu
from jax.sharding import PartitionSpec as P

STEPS = 6
RATE = 0.05
EPS = 1e-4
MESH = pl.DeviceIdType.MESH


def place(p, count):
    half = lax.div(p, 2)
    return jnp.where(lax.rem(p, 2) == 0, half, count - 1 - half)


def kernel(
    sizes, x_hbm, fj_hbm, fi_hbm, fk_hbm, std_hbm, end_hbm,
    field, flows, k_out, k_in, std, stat_out, stat_in,
    load_sem, k_send, k_recv, j_send, j_recv, i_send, i_recv, s_send, s_recv, end_sem, std_sem,
):
    n_j, n_i, n_k, n_lev = sizes
    south, east, down = (lax.axis_index(a) for a in ("south", "east", "down"))
    easts, downs = lax.axis_size("east"), lax.axis_size("down")
    has = {
        "k0": down > 0, "k1": down < downs - 1,
        "i0": east > 0, "i1": east < easts - 1,
    }
    near = {
        "k0": {"down": down - 1}, "k1": {"down": down + 1},
        "i0": {"east": east - 1}, "i1": {"east": east + 1},
        "j": {"south": 1 - south},
    }

    def load(a, p):
        i = place(p, n_i)
        src = (x_hbm, fj_hbm, fi_hbm, fk_hbm)[a].at[:, i]
        dst = field.at[0, i + 1, pl.ds(1, n_j)] if a == 0 else flows.at[a - 1, i]
        return pltpu.make_async_copy(src, dst, load_sem.at[a, p])

    for a in range(4):
        @pl.loop(0, n_i)
        def _(p):
            load(a, p).start()

    barrier = pltpu.get_barrier_semaphore()
    count = 1
    pl.semaphore_signal(barrier, inc=1, device_id=near["j"], device_id_type=MESH)
    for side in ("k0", "k1", "i0", "i1"):
        count = count + has[side].astype(jnp.int32)

        @pl.when(has[side])
        def _():
            pl.semaphore_signal(barrier, inc=1, device_id=near[side], device_id_type=MESH)

    nothing = jnp.zeros((8, n_k, n_lev), jnp.float32)
    for d in range(2):
        @pl.when(jnp.logical_not(has[f"k{d}"]))
        def _():
            @pl.loop(0, 2 * n_i)
            def _(q):
                k_in[lax.div(q, n_i), d, lax.rem(q, n_i)] = jnp.zeros((n_j, n_lev), jnp.float32)

        @pl.when(jnp.logical_not(has[f"i{d}"]))
        def _():
            @pl.loop(0, n_j // 8)
            def _(b):
                for par in range(2):
                    field[par, d * (n_i + 1), pl.ds(1 + b * 8, 8)] = nothing

        @pl.when(south == d)
        def _():
            @pl.loop(0, n_i)
            def _(i):
                for par in range(2):
                    field[par, i + 1, d * (n_j + 1)] = nothing[0]

    def k_copy(par, d, p):
        return pltpu.make_async_remote_copy(
            src_ref=k_out.at[par, d, p], dst_ref=k_in.at[par, 1 - d, p],
            send_sem=k_send.at[par, d, p], recv_sem=k_recv.at[par, 1 - d, p],
            device_id=near[f"k{d}"], device_id_type=MESH,
        )

    def k_arrival(par, d, p):
        return pltpu.make_async_remote_copy(
            src_ref=k_out.at[par, 1 - d, p], dst_ref=k_in.at[par, d, p],
            send_sem=k_send.at[par, 1 - d, p], recv_sem=k_recv.at[par, d, p],
            device_id=near[f"k{d}"], device_id_type=MESH,
        )

    def j_copy(par, p):
        i = place(p, n_i)
        return pltpu.make_async_remote_copy(
            src_ref=field.at[par, i + 1, jnp.where(south == 0, n_j, 1)],
            dst_ref=field.at[par, i + 1, jnp.where(south == 0, 0, n_j + 1)],
            send_sem=j_send.at[par, p], recv_sem=j_recv.at[par, p],
            device_id=near["j"], device_id_type=MESH,
        )

    def i_copy(par, d):
        return pltpu.make_async_remote_copy(
            src_ref=field.at[par, 1 + d * (n_i - 1), pl.ds(1, n_j)],
            dst_ref=field.at[par, (1 - d) * (n_i + 1), pl.ds(1, n_j)],
            send_sem=i_send.at[par, d], recv_sem=i_recv.at[par, 1 - d],
            device_id=near[f"i{d}"], device_id_type=MESH,
        )

    def i_arrival(par, d):
        return pltpu.make_async_remote_copy(
            src_ref=field.at[par, 1 + (1 - d) * (n_i - 1), pl.ds(1, n_j)],
            dst_ref=field.at[par, d * (n_i + 1), pl.ds(1, n_j)],
            send_sem=i_send.at[par, 1 - d], recv_sem=i_recv.at[par, d],
            device_id=near[f"i{d}"], device_id_type=MESH,
        )

    rows = field.reshape(2, n_i + 2, (n_j + 2) * n_k, n_lev)

    def extract(par, p):
        i = place(p, n_i)
        for d in range(2):
            k_out[par, d, p] = rows[par, i + 1, pl.ds(n_k + d * (n_k - 1), n_j, stride=n_k), :]

    def send(par, p):
        for d in range(2):
            @pl.when(has[f"k{d}"])
            def _():
                k_copy(par, d, p).start()
        j_copy(par, p).start()
        for d in range(2):
            @pl.when(jnp.logical_and(p == d, has[f"i{d}"]))
            def _():
                i_copy(par, d).start()

    def sent(par, p):
        for d in range(2):
            @pl.when(has[f"k{d}"])
            def _():
                k_copy(par, d, p).wait_send()
        j_copy(par, p).wait_send()
        for d in range(2):
            @pl.when(jnp.logical_and(p == d, has[f"i{d}"]))
            def _():
                i_copy(par, d).wait_send()

    def arrived(par, p):
        for d in range(2):
            @pl.when(has[f"k{d}"])
            def _():
                k_arrival(par, d, p).wait_recv()
        j_copy(par, p).wait_recv()
        for d in range(2):
            @pl.when(jnp.logical_and(p == d, has[f"i{d}"]))
            def _():
                i_arrival(par, d).wait_recv()

    level = lax.broadcasted_iota(jnp.int32, (n_k, n_lev), 0)
    first, last = level == 0, level == n_k - 1

    def advance(par, i, p, b, u):
        j = b * 8 + u
        mid = field[par, i + 1, j + 1]
        j0, j1 = field[par, i + 1, j], field[par, i + 1, j + 2]
        i0, i1 = field[par, i, j + 1], field[par, i + 2, j + 1]
        k0 = jnp.where(first, jnp.broadcast_to(k_in[par, 0, p, pl.ds(j, 1), :], (n_k, n_lev)), pltpu.roll(mid, 1, 0))
        k1 = jnp.where(last, jnp.broadcast_to(k_in[par, 1, p, pl.ds(j, 1), :], (n_k, n_lev)), pltpu.roll(mid, n_k - 1, 0))
        around = ((j0 + j1) + (i0 + i1)) + (k0 + k1)
        kept = (1.0 - 6.0 * RATE) * mid + RATE * around
        return kept - flows[0, i, j] * (j1 - j0) - flows[1, i, j] * (i1 - i0) - flows[2, i, j] * (k1 - k0)

    @pl.loop(0, n_i)
    def _(p):
        load(0, p).wait()
        extract(0, p)

    pl.semaphore_wait(barrier, count)

    @pl.loop(0, n_i)
    def _(p):
        send(0, p)

    @pl.loop(0, STEPS - 1)
    def _(n):
        par = lax.rem(n, 2)

        @pl.loop(0, n_i)
        def _(p):
            i = place(p, n_i)

            @pl.when(n == 0)
            def _():
                for a in range(1, 4):
                    load(a, p).wait()

            arrived(par, p)

            @pl.when(n > 0)
            def _():
                sent(1 - par, p)

            @pl.loop(0, n_j // 8)
            def _(b):
                for u in range(8):
                    field[1 - par, i + 1, b * 8 + u + 1] = advance(par, i, p, b, u)

            extract(1 - par, p)
            send(1 - par, p)

    par = (STEPS - 1) % 2
    fin = 1 - par

    def stat_copy(p):
        return pltpu.make_async_remote_copy(
            src_ref=stat_out.at[p], dst_ref=stat_in.at[p],
            send_sem=s_send.at[p], recv_sem=s_recv.at[p],
            device_id=near["j"], device_id_type=MESH,
        )

    def end_copy(p):
        i = place(p, n_i)
        return pltpu.make_async_copy(field.at[fin, i + 1, pl.ds(1, n_j)], end_hbm.at[:, i], end_sem.at[p])

    def std_copy(p):
        i = place(p, n_i)
        return pltpu.make_async_copy(std.at[i], std_hbm.at[:, i], std_sem.at[p])

    def finish(p):
        i = place(p, n_i)
        stat_copy(p).wait_recv()
        mine, other = stat_out[p, 0], stat_in[p, 0]
        gap = mine - other
        mean = 0.5 * (mine + other)
        squares = stat_out[p, 1] + stat_in[p, 1] + (0.5 * n_j) * (gap * gap)
        scale = lax.rsqrt(squares * (0.5 / n_j) + EPS)

        @pl.loop(0, n_j // 8)
        def _(b):
            for u in range(8):
                j = b * 8 + u
                std[i, j] = (field[fin, i + 1, j + 1] - mean) * scale

        std_copy(p).start()

    @pl.loop(0, n_i)
    def _(p):
        i = place(p, n_i)
        arrived(par, p)
        sent(fin, p)

        def ahead(b, total):
            parts = []
            for u in range(8):
                new = advance(par, i, p, b, u)
                field[fin, i + 1, b * 8 + u + 1] = new
                parts.append(new)
            while len(parts) > 1:
                parts = [a + c for a, c in zip(parts[::2], parts[1::2])]
            return total + parts[0]

        total = lax.fori_loop(0, n_j // 8, ahead, jnp.zeros((n_k, n_lev), jnp.float32))
        end_copy(p).start()
        mean = total * (1.0 / n_j)

        def spread(b, total):
            parts = []
            for u in range(8):
                off = field[fin, i + 1, b * 8 + u + 1] - mean
                parts.append(off * off)
            while len(parts) > 1:
                parts = [a + c for a, c in zip(parts[::2], parts[1::2])]
            return total + parts[0]

        stat_out[p, 0] = mean
        stat_out[p, 1] = lax.fori_loop(0, n_j // 8, spread, jnp.zeros((n_k, n_lev), jnp.float32))
        stat_copy(p).start()

        @pl.when(p > 0)
        def _():
            finish(p - 1)

    finish(n_i - 1)

    @pl.loop(0, n_i)
    def _(p):
        sent(par, p)
        stat_copy(p).wait_send()
        end_copy(p).wait()
        std_copy(p).wait()


def per_device(field_values, flow_j, flow_i, flow_k):
    n_j, n_i, n_k, n_lev = sizes = field_values.shape
    f32, dma = jnp.float32, pltpu.SemaphoreType.DMA
    out = jax.ShapeDtypeStruct(sizes, f32)
    anywhere = pl.BlockSpec(memory_space=pl.ANY)
    return pl.pallas_call(
        functools.partial(kernel, sizes),
        out_shape=(out, out),
        in_specs=[anywhere] * 4,
        out_specs=(anywhere, anywhere),
        scratch_shapes=[
            pltpu.VMEM((2, n_i + 2, n_j + 2, n_k, n_lev), f32),
            pltpu.VMEM((3, n_i, n_j, n_k, n_lev), f32),
            pltpu.VMEM((2, 2, n_i, n_j, n_lev), f32),
            pltpu.VMEM((2, 2, n_i, n_j, n_lev), f32),
            pltpu.VMEM((n_i, n_j, n_k, n_lev), f32),
            pltpu.VMEM((n_i, 2, n_k, n_lev), f32),
            pltpu.VMEM((n_i, 2, n_k, n_lev), f32),
            dma((4, n_i)),
            dma((2, 2, n_i)), dma((2, 2, n_i)),
            dma((2, n_i)), dma((2, n_i)),
            dma((2, 2)), dma((2, 2)),
            dma((n_i,)), dma((n_i,)),
            dma((n_i,)), dma((n_i,)),
        ],
        compiler_params=pltpu.CompilerParams(
            collective_id=0, has_side_effects=True, vmem_limit_bytes=60 * 1024 * 1024
        ),
        name="transport",
    )(field_values, flow_j, flow_i, flow_k)


def solution(mesh):
    spec = P("south", "east", "down", None)
    return jax.shard_map(
        per_device, mesh=mesh, in_specs=(spec,) * 4, out_specs=(spec, spec), check_vma=False
    )
```

time: 295 us -> 169 us (0.57)
  Pallas kernels: 0 us -> 161 us
  starting transfers between devices: 107 us -> 0 us
  waiting for transfers between devices: 96.5 us -> 0 us
  other arithmetic: 66.7 us -> 0 us
  blocking collectives: 8.44 us -> 0 us
  local copies, waits for them, and re-layouts: 13.7 us -> 6.96 us
    pallas_call x0 -> x1, Pallas kernels: none -> 161 us  [per_device(): pl.pallas_call(functools.partial(kernel, sizes), out_shape=(out, out), in...]
    ppermute x36 -> x0, starting transfers between devices: 107 us -> none  [the longest x18 72.5 us: with_halo(): lax.ppermute(last, axis, up)]
    ppermute x36 -> x0, waiting for transfers between devices: 96.5 us -> none  [the longest x18 81.6 us: with_halo(): lax.ppermute(leading, axis, [(b, a) for a, b in up])]
    add x6 -> x0, other arithmetic: 50.3 us -> none  [the longest x5 50.3 us: advance(): middle - flow_j * slopes[0] - flow_i * slopes[1] - flow_k * slopes[2]]
    reduce_sum x2 -> x0, other arithmetic: 11.3 us -> none  [the longest x1 11.1 us: per_device(): jnp.sum(moved, axis=0, keepdims=True)]
    slice x18 -> x0, local copies, waits for them, and re-layouts: 10.5 us -> none  [the longest x16 9.09 us: with_halo(): last = lax.slice_in_dim(shard, length - width, length, axis=dim)]
    all_to_all x1 -> x0, blocking collectives: 8.44 us -> none  [sent_to_all(): lax.all_to_all(jnp.broadcast_to(shard[None], (devices, *shard.shape)), ax...]
    mul x1 -> x0, other arithmetic: 5.13 us -> none  [per_device(): standardized = centred * lax.rsqrt(line_variance + 0.0001)]
  transfers between devices with their start and end apart: 36 -> 0, of which waited for: 7 -> 0; matrix products, arithmetic and copies ran while one was open for 4% -> 0% of each run, Pallas kernels for 0% -> 0%
where the time goes in v1:
time: 169 us
  Pallas kernels  161 us (95%)
  local copies, waits for them, and re-layouts  6.96 us (4%)
    pallas_call x1, Pallas kernels, per_device(): pl.pallas_call(functools.partial(kernel, sizes), out_shape=(out, out), in...  161 us
    unnamed x4, local copies, waits for them, and re-layouts  6.96 us

profile of v1, /device:TPU:96, one launch (start us, length us, event | category | flops | bytes accessed | tf_op | source)
XLA Modules:
  0.0 168.8 jit_solution(1680430636827216832)
XLA Ops:
  0.6 161.2 %transport.1 = (f32[128,8,8,128]{3,2,1,0:T(8,128)}, f32[128,8,8,128]{3,2,1,0:T(8,128)}) custom-call(f32[128,8,8,128]{3,2,1,0:T(8,128)} %x_hbm.1, f32[128,8,8,128]{3,2,1,0:T(8,128)} %fj_hbm.1, f32[128,8,8,128]{3,2,1,0:T(8,128)} %fi_hbm.1, f32[128,8,8,128]{3,2,1,0:T(8,128)} %fk_hbm.1), custom_call_target="tpu_custom_call" | custom-call | tf_op jit(solution)/shard_map/transport/pallas_call | solution.py:300
  161.8 0.0 copy-start
  161.8 4.9 %copy.8 = f32[128,8,8,128]{3,2,1,0:T(8,128)} copy(f32[128,8,8,128]{3,2,1,0:T(8,128)} %get-tuple-element.4) | data formatting | bytes 8388608
  166.7 0.0 copy-done
  166.7 2.0 %copy.9 = f32[128,8,8,128]{3,2,1,0:T(8,128)} copy(f32[128,8,8,128]{3,2,1,0:T(8,128)S(1)} %copy-done) | data formatting | bytes 8388608
Async XLA Ops:
  161.8 5.0 %copy-start = (f32[128,8,8,128]{3,2,1,0:T(8,128)S(1)}, f32[128,8,8,128]{3,2,1,0:T(8,128)}, u32[]{:S(2)}) copy-start(f32[128,8,8,128]{3,2,1,0:T(8,128)} %get-tuple-element.5) | copy-start | bytes 12582916

commit v2 on v1

--- a/solution.py
+++ b/solution.py
@@ -10,6 +10,7 @@
 STEPS = 6
 RATE = 0.05
 EPS = 1e-4
+LAG = 1
 MESH = pl.DeviceIdType.MESH
 
 
@@ -19,9 +20,9 @@
 
 
 def kernel(
-    sizes, x_hbm, fj_hbm, fi_hbm, fk_hbm, std_hbm, end_hbm,
-    field, flows, k_out, k_in, std, stat_out, stat_in,
-    load_sem, k_send, k_recv, j_send, j_recv, i_send, i_recv, s_send, s_recv, end_sem, std_sem,
+    sizes, x_hbm, fj_hbm, fi_hbm, fk_hbm, std, end,
+    field, flows, k_out, k_in, passing, stat_out, stat_in,
+    load_sem, k_send, k_recv, p_send, p_recv, j_send, j_recv, i_send, i_recv, s_send, s_recv,
 ):
     n_j, n_i, n_k, n_lev = sizes
     south, east, down = (lax.axis_index(a) for a in ("south", "east", "down"))
@@ -29,12 +30,51 @@
     has = {
         "k0": down > 0, "k1": down < downs - 1,
         "i0": east > 0, "i1": east < easts - 1,
+        "p0": down > 1, "p1": down < downs - 2,
     }
     near = {
         "k0": {"down": down - 1}, "k1": {"down": down + 1},
         "i0": {"east": east - 1}, "i1": {"east": east + 1},
+        "p0": {"down": down - 2}, "p1": {"down": down + 2},
         "j": {"south": 1 - south},
     }
+    odd = lax.rem(down, 2) == 1
+    slant = (jnp.logical_and(jnp.logical_not(odd), has["k0"]), jnp.logical_and(odd, has["k1"]))
+
+    def passed(sender, p):
+        straight = lax.div(n_i * jnp.where(odd, downs - 1 - sender, sender), downs)
+        return lax.div((p + 1) * straight, n_i) == lax.div(p * straight, n_i)
+
+    passer = jnp.where(odd, down > 1, down < downs - 2)
+    pass_from = jnp.where(odd, down - 2, down + 2)
+    pass_side = jnp.where(odd, 0, 1)
+
+    def pass_copy(n, p):
+        par = lax.rem(n, 2)
+        return pltpu.make_async_remote_copy(
+            src_ref=passing.at[n, p], dst_ref=k_in.at[par, pass_side, p],
+            send_sem=p_send.at[par, p], recv_sem=k_recv.at[par, pass_side, p],
+            device_id={"down": jnp.where(odd, down - 1, down + 1)}, device_id_type=MESH,
+        )
+
+    def pass_arrival(n, p):
+        par = lax.rem(n, 2)
+        return pltpu.make_async_remote_copy(
+            src_ref=k_out.at[par, 0, p], dst_ref=passing.at[n, p],
+            send_sem=p_send.at[par, p], recv_sem=p_recv.at[par, p],
+            device_id={"down": pass_from}, device_id_type=MESH,
+        )
+
+    def pass_on(n, p):
+        @pl.when(jnp.logical_and(passer, passed(pass_from, p)))
+        def _():
+            pass_arrival(n, p).wait_recv()
+
+            @pl.when(n >= 2)
+            def _():
+                pass_copy(n - 2, p).wait_send()
+
+            pass_copy(n, p).start()
 
     def load(a, p):
         i = place(p, n_i)
@@ -50,7 +90,7 @@
     barrier = pltpu.get_barrier_semaphore()
     count = 1
     pl.semaphore_signal(barrier, inc=1, device_id=near["j"], device_id_type=MESH)
-    for side in ("k0", "k1", "i0", "i1"):
+    for side in ("k0", "k1", "i0", "i1", "p0", "p1"):
         count = count + has[side].astype(jnp.int32)
 
         @pl.when(has[side])
@@ -86,6 +126,14 @@
             device_id=near[f"k{d}"], device_id_type=MESH,
         )
 
+    def k_slant(n, d, p):
+        par = lax.rem(n, 2)
+        return pltpu.make_async_remote_copy(
+            src_ref=k_out.at[par, d, p], dst_ref=passing.at[n, p],
+            send_sem=k_send.at[par, d, p], recv_sem=p_recv.at[par, p],
+            device_id=near[f"p{d}"], device_id_type=MESH,
+        )
+
     def k_arrival(par, d, p):
         return pltpu.make_async_remote_copy(
             src_ref=k_out.at[par, 1 - d, p], dst_ref=k_in.at[par, d, p],
@@ -125,9 +173,15 @@
         for d in range(2):
             k_out[par, d, p] = rows[par, i + 1, pl.ds(n_k + d * (n_k - 1), n_j, stride=n_k), :]
 
-    def send(par, p):
-        for d in range(2):
-            @pl.when(has[f"k{d}"])
+    def send(n, p):
+        par = lax.rem(n, 2)
+        around = passed(down, p)
+        for d in range(2):
+            @pl.when(jnp.logical_and(slant[d], around))
+            def _():
+                k_slant(n, d, p).start()
+
+            @pl.when(jnp.logical_and(has[f"k{d}"], jnp.logical_not(jnp.logical_and(slant[d], around))))
             def _():
                 k_copy(par, d, p).start()
         j_copy(par, p).start()
@@ -183,6 +237,10 @@
     def _(p):
         send(0, p)
 
+    @pl.loop(0, n_i - LAG)
+    def _(p):
+        pass_on(0, p)
+
     @pl.loop(0, STEPS - 1)
     def _(n):
         par = lax.rem(n, 2)
@@ -208,7 +266,9 @@
                     field[1 - par, i + 1, b * 8 + u + 1] = advance(par, i, p, b, u)
 
             extract(1 - par, p)
-            send(1 - par, p)
+            send(n + 1, p)
+            at = (n + 1) * n_i + p - LAG
+            pass_on(lax.div(at, n_i), lax.rem(at, n_i))
 
     par = (STEPS - 1) % 2
     fin = 1 - par
@@ -219,14 +279,6 @@
             send_sem=s_send.at[p], recv_sem=s_recv.at[p],
             device_id=near["j"], device_id_type=MESH,
         )
-
-    def end_copy(p):
-        i = place(p, n_i)
-        return pltpu.make_async_copy(field.at[fin, i + 1, pl.ds(1, n_j)], end_hbm.at[:, i], end_sem.at[p])
-
-    def std_copy(p):
-        i = place(p, n_i)
-        return pltpu.make_async_copy(std.at[i], std_hbm.at[:, i], std_sem.at[p])
 
     def finish(p):
         i = place(p, n_i)
@@ -241,13 +293,16 @@
         def _(b):
             for u in range(8):
                 j = b * 8 + u
-                std[i, j] = (field[fin, i + 1, j + 1] - mean) * scale
-
-        std_copy(p).start()
+                std[j, i] = (end[j, i] - mean) * scale
 
     @pl.loop(0, n_i)
     def _(p):
         i = place(p, n_i)
+
+        @pl.when(p < LAG)
+        def _():
+            pass_on(STEPS - 1, n_i - LAG + p)
+
         arrived(par, p)
         sent(fin, p)
 
@@ -255,20 +310,19 @@
             parts = []
             for u in range(8):
                 new = advance(par, i, p, b, u)
-                field[fin, i + 1, b * 8 + u + 1] = new
+                end[b * 8 + u, i] = new
                 parts.append(new)
             while len(parts) > 1:
                 parts = [a + c for a, c in zip(parts[::2], parts[1::2])]
             return total + parts[0]
 
         total = lax.fori_loop(0, n_j // 8, ahead, jnp.zeros((n_k, n_lev), jnp.float32))
-        end_copy(p).start()
         mean = total * (1.0 / n_j)
 
         def spread(b, total):
             parts = []
             for u in range(8):
-                off = field[fin, i + 1, b * 8 + u + 1] - mean
+                off = end[b * 8 + u, i] - mean
                 parts.append(off * off)
             while len(parts) > 1:
                 parts = [a + c for a, c in zip(parts[::2], parts[1::2])]
@@ -287,9 +341,13 @@
     @pl.loop(0, n_i)
     def _(p):
         sent(par, p)
+
+        @pl.when(jnp.logical_and(passer, passed(pass_from, p)))
+        def _():
+            for n in (STEPS - 2, STEPS - 1):
+                pass_copy(n, p).wait_send()
+
         stat_copy(p).wait_send()
-        end_copy(p).wait()
-        std_copy(p).wait()
 
 
 def per_device(field_values, flow_j, flow_i, flow_k):
@@ -301,24 +359,24 @@
         functools.partial(kernel, sizes),
         out_shape=(out, out),
         in_specs=[anywhere] * 4,
-        out_specs=(anywhere, anywhere),
+        out_specs=(pl.BlockSpec(memory_space=pltpu.VMEM),) * 2,
         scratch_shapes=[
             pltpu.VMEM((2, n_i + 2, n_j + 2, n_k, n_lev), f32),
             pltpu.VMEM((3, n_i, n_j, n_k, n_lev), f32),
             pltpu.VMEM((2, 2, n_i, n_j, n_lev), f32),
             pltpu.VMEM((2, 2, n_i, n_j, n_lev), f32),
-            pltpu.VMEM((n_i, n_j, n_k, n_lev), f32),
+            pltpu.VMEM((STEPS, n_i, n_j, n_lev), f32),
             pltpu.VMEM((n_i, 2, n_k, n_lev), f32),
             pltpu.VMEM((n_i, 2, n_k, n_lev), f32),
             dma((4, n_i)),
             dma((2, 2, n_i)), dma((2, 2, n_i)),
             dma((2, n_i)), dma((2, n_i)),
+            dma((2, n_i)), dma((2, n_i)),
             dma((2, 2)), dma((2, 2)),
-            dma((n_i,)), dma((n_i,)),
             dma((n_i,)), dma((n_i,)),
         ],
         compiler_params=pltpu.CompilerParams(
-            collective_id=0, has_side_effects=True, vmem_limit_bytes=60 * 1024 * 1024
+            collective_id=0, has_side_effects=True, vmem_limit_bytes=44 * 1024 * 1024
         ),
         name="transport",
     )(field_values, flow_j, flow_i, flow_k)

time: 169 us -> 151 us (0.89)
  Pallas kernels: 161 us -> 144 us
  local copies, waits for them, and re-layouts: 6.96 us -> 4.03 us
    pallas_call x1, Pallas kernels: 161 us -> 144 us  [per_device(): pl.pallas_call(functools.partial(kernel, sizes), out_shape=(out, out), in...]
    unnamed x4 -> x2, local copies, waits for them, and re-layouts: 6.96 us -> 4.03 us
where the time goes in v2:
time: 151 us; the launch traced here: 149 us
  Pallas kernels  144 us (95%)
  local copies, waits for them, and re-layouts  4.03 us (3%)
    pallas_call x1, Pallas kernels, per_device(): pl.pallas_call(functools.partial(kernel, sizes), out_shape=(out, out), in...  144 us
    unnamed x2, local copies, waits for them, and re-layouts  4.03 us

profile of v2, /device:TPU:96, one launch (start us, length us, event | category | flops | bytes accessed | tf_op | source)
XLA Modules:
  0.0 149.1 jit_solution(1764804755309073432)
XLA Ops:
  0.6 144.5 %transport.1 = (f32[128,8,8,128]{3,2,1,0:T(8,128)S(1)}, f32[128,8,8,128]{3,2,1,0:T(8,128)S(1)}) custom-call(f32[128,8,8,128]{3,2,1,0:T(8,128)} %x_hbm.1, f32[128,8,8,128]{3,2,1,0:T(8,128)} %fj_hbm.1, f32[128,8,8,128]{3,2,1,0:T(8,128)} %fi_hbm.1, f32[128,8,8,128]{3,2,1,0:T(8,128)} %fk_hbm.1), custom_call_target="tpu_custom_call" | custom-call | tf_op jit(solution)/shard_map/transport/pallas_call | solution.py:358
  145.1 2.0 %copy.8 = f32[128,8,8,128]{3,2,1,0:T(8,128)} copy(f32[128,8,8,128]{3,2,1,0:T(8,128)S(1)} %get-tuple-element.4) | data formatting | bytes 8388608
  147.1 2.0 %copy.9 = f32[128,8,8,128]{3,2,1,0:T(8,128)} copy(f32[128,8,8,128]{3,2,1,0:T(8,128)S(1)} %get-tuple-element.5) | data formatting | bytes 8388608

commit v3 on v2

--- a/solution.py
+++ b/solution.py
@@ -262,8 +262,9 @@
 
             @pl.loop(0, n_j // 8)
             def _(b):
+                new = [advance(par, i, p, b, u) for u in range(8)]
                 for u in range(8):
-                    field[1 - par, i + 1, b * 8 + u + 1] = advance(par, i, p, b, u)
+                    field[1 - par, i + 1, b * 8 + u + 1] = new[u]
 
             extract(1 - par, p)
             send(n + 1, p)
@@ -291,9 +292,9 @@
 
         @pl.loop(0, n_j // 8)
         def _(b):
+            done = [(end[b * 8 + u, i] - mean) * scale for u in range(8)]
             for u in range(8):
-                j = b * 8 + u
-                std[j, i] = (end[j, i] - mean) * scale
+                std[b * 8 + u, i] = done[u]
 
     @pl.loop(0, n_i)
     def _(p):
@@ -307,11 +308,9 @@
         sent(fin, p)
 
         def ahead(b, total):
-            parts = []
+            parts = [advance(par, i, p, b, u) for u in range(8)]
             for u in range(8):
-                new = advance(par, i, p, b, u)
-                end[b * 8 + u, i] = new
-                parts.append(new)
+                end[b * 8 + u, i] = parts[u]
             while len(parts) > 1:
                 parts = [a + c for a, c in zip(parts[::2], parts[1::2])]
             return total + parts[0]
@@ -332,11 +331,9 @@
         stat_out[p, 1] = lax.fori_loop(0, n_j // 8, spread, jnp.zeros((n_k, n_lev), jnp.float32))
         stat_copy(p).start()
 
-        @pl.when(p > 0)
-        def _():
-            finish(p - 1)
-
-    finish(n_i - 1)
+    @pl.loop(0, n_i)
+    def _(p):
+        finish(p)
 
     @pl.loop(0, n_i)
     def _(p):

time: 151 us -> 140 us (0.927); the launches traced: 149 us -> 140 us
  Pallas kernels: 144 us -> 135 us
    pallas_call x1, Pallas kernels: 144 us -> 135 us  [per_device(): pl.pallas_call(functools.partial(kernel, sizes), out_shape=(out, out), in...]
where the time goes in v3:
time: 140 us
  Pallas kernels  135 us (96%)
  local copies, waits for them, and re-layouts  4.03 us (3%)
    pallas_call x1, Pallas kernels, per_device(): pl.pallas_call(functools.partial(kernel, sizes), out_shape=(out, out), in...  135 us
    unnamed x2, local copies, waits for them, and re-layouts  4.03 us

profile of v3, /device:TPU:96, one launch (start us, length us, event | category | flops | bytes accessed | tf_op | source)
XLA Modules:
  0.0 140.1 jit_solution(11650203343319972563)
XLA Ops:
  0.6 135.4 %transport.1 = (f32[128,8,8,128]{3,2,1,0:T(8,128)S(1)}, f32[128,8,8,128]{3,2,1,0:T(8,128)S(1)}) custom-call(f32[128,8,8,128]{3,2,1,0:T(8,128)} %x_hbm.1, f32[128,8,8,128]{3,2,1,0:T(8,128)} %fj_hbm.1, f32[128,8,8,128]{3,2,1,0:T(8,128)} %fi_hbm.1, f32[128,8,8,128]{3,2,1,0:T(8,128)} %fk_hbm.1), custom_call_target="tpu_custom_call" | custom-call | tf_op jit(solution)/shard_map/transport/pallas_call | solution.py:355
  136.0 2.0 %copy.8 = f32[128,8,8,128]{3,2,1,0:T(8,128)} copy(f32[128,8,8,128]{3,2,1,0:T(8,128)S(1)} %get-tuple-element.4) | data formatting | bytes 8388608
  138.1 2.0 %copy.9 = f32[128,8,8,128]{3,2,1,0:T(8,128)} copy(f32[128,8,8,128]{3,2,1,0:T(8,128)S(1)} %get-tuple-element.5) | data formatting | bytes 8388608

commit v4 on v3

--- a/solution.py
+++ b/solution.py
@@ -11,6 +11,7 @@
 RATE = 0.05
 EPS = 1e-4
 LAG = 1
+FIRST_LAG = 2
 MESH = pl.DeviceIdType.MESH
 
 
@@ -43,7 +44,8 @@
 
     def passed(sender, p):
         straight = lax.div(n_i * jnp.where(odd, downs - 1 - sender, sender), downs)
-        return lax.div((p + 1) * straight, n_i) == lax.div(p * straight, n_i)
+        shift = jnp.where(2 * straight > n_i, n_i - straight, 0)
+        return lax.div((p + 1) * straight + shift, n_i) == lax.div(p * straight + shift, n_i)
 
     passer = jnp.where(odd, down > 1, down < downs - 2)
     pass_from = jnp.where(odd, down - 2, down + 2)
@@ -82,10 +84,8 @@
         dst = field.at[0, i + 1, pl.ds(1, n_j)] if a == 0 else flows.at[a - 1, i]
         return pltpu.make_async_copy(src, dst, load_sem.at[a, p])
 
-    for a in range(4):
-        @pl.loop(0, n_i)
-        def _(p):
-            load(a, p).start()
+    for p in range(n_i):
+        load(0, p).start()
 
     barrier = pltpu.get_barrier_semaphore()
     count = 1
@@ -96,28 +96,6 @@
         @pl.when(has[side])
         def _():
             pl.semaphore_signal(barrier, inc=1, device_id=near[side], device_id_type=MESH)
-
-    nothing = jnp.zeros((8, n_k, n_lev), jnp.float32)
-    for d in range(2):
-        @pl.when(jnp.logical_not(has[f"k{d}"]))
-        def _():
-            @pl.loop(0, 2 * n_i)
-            def _(q):
-                k_in[lax.div(q, n_i), d, lax.rem(q, n_i)] = jnp.zeros((n_j, n_lev), jnp.float32)
-
-        @pl.when(jnp.logical_not(has[f"i{d}"]))
-        def _():
-            @pl.loop(0, n_j // 8)
-            def _(b):
-                for par in range(2):
-                    field[par, d * (n_i + 1), pl.ds(1 + b * 8, 8)] = nothing
-
-        @pl.when(south == d)
-        def _():
-            @pl.loop(0, n_i)
-            def _(i):
-                for par in range(2):
-                    field[par, i + 1, d * (n_j + 1)] = nothing[0]
 
     def k_copy(par, d, p):
         return pltpu.make_async_remote_copy(
@@ -226,18 +204,49 @@
         kept = (1.0 - 6.0 * RATE) * mid + RATE * around
         return kept - flows[0, i, j] * (j1 - j0) - flows[1, i, j] * (i1 - i0) - flows[2, i, j] * (k1 - k0)
 
-    @pl.loop(0, n_i)
+    load(0, 0).wait()
+    extract(0, 0)
+    pl.semaphore_wait(barrier, count)
+    send(0, 0)
+
+    @pl.loop(1, n_i)
     def _(p):
         load(0, p).wait()
         extract(0, p)
-
-    pl.semaphore_wait(barrier, count)
+        send(0, p)
+
+        @pl.when(p >= FIRST_LAG)
+        def _():
+            pass_on(0, p - FIRST_LAG)
 
     @pl.loop(0, n_i)
     def _(p):
-        send(0, p)
-
-    @pl.loop(0, n_i - LAG)
+        for a in range(1, 4):
+            load(a, p).start()
+
+    nothing = jnp.zeros((8, n_k, n_lev), jnp.float32)
+    for d in range(2):
+        @pl.when(jnp.logical_not(has[f"k{d}"]))
+        def _():
+            @pl.loop(0, 2 * n_i)
+            def _(q):
+                k_in[lax.div(q, n_i), d, lax.rem(q, n_i)] = jnp.zeros((n_j, n_lev), jnp.float32)
+
+        @pl.when(jnp.logical_not(has[f"i{d}"]))
+        def _():
+            @pl.loop(0, n_j // 8)
+            def _(b):
+                for par in range(2):
+                    field[par, d * (n_i + 1), pl.ds(1 + b * 8, 8)] = nothing
+
+        @pl.when(south == d)
+        def _():
+            @pl.loop(0, n_i)
+            def _(i):
+                for par in range(2):
+                    field[par, i + 1, d * (n_j + 1)] = nothing[0]
+
+    @pl.loop(n_i - FIRST_LAG, n_i - LAG)
     def _(p):
         pass_on(0, p)
 
@@ -347,12 +356,26 @@
         stat_copy(p).wait_send()
 
 
+def write_out(std, end, std_hbm, end_hbm, sem):
+    parts = sem.shape[1]
+    size = std.shape[0] // parts
+    copies = [
+        pltpu.make_async_copy(src.at[pl.ds(b * size, size)], dst.at[pl.ds(b * size, size)], sem.at[a, b])
+        for b in range(parts)
+        for a, (src, dst) in enumerate(((end, end_hbm), (std, std_hbm)))
+    ]
+    for copy in copies:
+        copy.start()
+    for copy in copies:
+        copy.wait()
+
+
 def per_device(field_values, flow_j, flow_i, flow_k):
     n_j, n_i, n_k, n_lev = sizes = field_values.shape
     f32, dma = jnp.float32, pltpu.SemaphoreType.DMA
     out = jax.ShapeDtypeStruct(sizes, f32)
     anywhere = pl.BlockSpec(memory_space=pl.ANY)
-    return pl.pallas_call(
+    std, end = pl.pallas_call(
         functools.partial(kernel, sizes),
         out_shape=(out, out),
         in_specs=[anywhere] * 4,
@@ -377,6 +400,15 @@
         ),
         name="transport",
     )(field_values, flow_j, flow_i, flow_k)
+    return pl.pallas_call(
+        write_out,
+        out_shape=(out, out),
+        in_specs=[pl.BlockSpec(memory_space=pltpu.VMEM)] * 2,
+        out_specs=(anywhere, anywhere),
+        scratch_shapes=[dma((2, 4))],
+        compiler_params=pltpu.CompilerParams(vmem_limit_bytes=1024 * 1024),
+        name="write_out",
+    )(std, end)
 
 
 def solution(mesh):

time: 140 us -> 139 us (level)
  local copies, waits for them, and re-layouts: 4.03 us -> 0 us
  Pallas kernels: 135 us -> 138 us
    unnamed x2 -> x0, local copies, waits for them, and re-layouts: 4.03 us -> none
    pallas_call x0 -> x1, Pallas kernels: none -> 3.37 us  [per_device(): pl.pallas_call(write_out, out_shape=(out, out), in_specs=[pl.BlockSpec(me...]
where the time goes in v4:
time: 139 us
  Pallas kernels  138 us (99%)
    pallas_call x1, Pallas kernels, per_device(): pl.pallas_call(functools.partial(kernel, sizes), out_shape=(out, out), in...  135 us
    pallas_call x1, Pallas kernels, per_device(): pl.pallas_call(write_out, out_shape=(out, out), in_specs=[pl.BlockSpec(me...  3.37 us

profile of v4, /device:TPU:96, one launch (start us, length us, event | category | flops | bytes accessed | tf_op | source)
XLA Modules:
  0.0 138.8 jit_solution(11334199577379411644)
XLA Ops:
  0.6 134.8 %transport.1 = (f32[128,8,8,128]{3,2,1,0:T(8,128)S(1)}, f32[128,8,8,128]{3,2,1,0:T(8,128)S(1)}) custom-call(f32[128,8,8,128]{3,2,1,0:T(8,128)} %x_hbm.1, f32[128,8,8,128]{3,2,1,0:T(8,128)} %fj_hbm.1, f32[128,8,8,128]{3,2,1,0:T(8,128)} %fi_hbm.1, f32[128,8,8,128]{3,2,1,0:T(8,128)} %fk_hbm.1), custom_call_target="tpu_custom_call" | custom-call | tf_op jit(solution)/shard_map/transport/pallas_call | solution.py:378
  135.5 3.4 %write_out.1 = (f32[128,8,8,128]{3,2,1,0:T(8,128)}, f32[128,8,8,128]{3,2,1,0:T(8,128)}) custom-call(f32[128,8,8,128]{3,2,1,0:T(8,128)S(1)} %get-tuple-element.4.std, f32[128,8,8,128]{3,2,1,0:T(8,128)S(1)} %get-tuple-element.5.end), custom_call_target="tpu_custom_call" | custom-call | tf_op jit(solution)/shard_map/write_out/pallas_call | solution.py:403

commit v5 on v4

--- a/solution.py
+++ b/solution.py
@@ -159,6 +159,7 @@
             def _():
                 k_slant(n, d, p).start()
 
+        for d in range(2):
             @pl.when(jnp.logical_and(has[f"k{d}"], jnp.logical_not(jnp.logical_and(slant[d], around))))
             def _():
                 k_copy(par, d, p).start()
@@ -276,9 +277,9 @@
                     field[1 - par, i + 1, b * 8 + u + 1] = new[u]
 
             extract(1 - par, p)
-            send(n + 1, p)
             at = (n + 1) * n_i + p - LAG
             pass_on(lax.div(at, n_i), lax.rem(at, n_i))
+            send(n + 1, p)
 
     par = (STEPS - 1) % 2
     fin = 1 - par

time: 139 us -> 139 us (level)
  no operation moved by 1% of the time
where the time goes in v5:
time: 139 us; the launch traced here: 138 us
  Pallas kernels  138 us (99%)
    pallas_call x1, Pallas kernels, per_device(): pl.pallas_call(functools.partial(kernel, sizes), out_shape=(out, out), in...  134 us
    pallas_call x1, Pallas kernels, per_device(): pl.pallas_call(write_out, out_shape=(out, out), in_specs=[pl.BlockSpec(me...  3.37 us

profile of v5, /device:TPU:96, one launch (start us, length us, event | category | flops | bytes accessed | tf_op | source)
XLA Modules:
  0.0 138.2 jit_solution(3279281702471526003)
XLA Ops:
  0.6 134.2 %transport.1 = (f32[128,8,8,128]{3,2,1,0:T(8,128)S(1)}, f32[128,8,8,128]{3,2,1,0:T(8,128)S(1)}) custom-call(f32[128,8,8,128]{3,2,1,0:T(8,128)} %x_hbm.1, f32[128,8,8,128]{3,2,1,0:T(8,128)} %fj_hbm.1, f32[128,8,8,128]{3,2,1,0:T(8,128)} %fi_hbm.1, f32[128,8,8,128]{3,2,1,0:T(8,128)} %fk_hbm.1), custom_call_target="tpu_custom_call" | custom-call | tf_op jit(solution)/shard_map/transport/pallas_call | solution.py:379
  134.9 3.4 %write_out.1 = (f32[128,8,8,128]{3,2,1,0:T(8,128)}, f32[128,8,8,128]{3,2,1,0:T(8,128)}) custom-call(f32[128,8,8,128]{3,2,1,0:T(8,128)S(1)} %get-tuple-element.4.std, f32[128,8,8,128]{3,2,1,0:T(8,128)S(1)} %get-tuple-element.5.end), custom_call_target="tpu_custom_call" | custom-call | tf_op jit(solution)/shard_map/write_out/pallas_call | solution.py:404

commit v6 on v5

--- a/solution.py
+++ b/solution.py
@@ -264,6 +264,8 @@
                 for a in range(1, 4):
                     load(a, p).wait()
 
+            at = (n + 1) * n_i + p - LAG
+            pass_on(lax.div(at, n_i), lax.rem(at, n_i))
             arrived(par, p)
 
             @pl.when(n > 0)
@@ -277,8 +279,6 @@
                     field[1 - par, i + 1, b * 8 + u + 1] = new[u]
 
             extract(1 - par, p)
-            at = (n + 1) * n_i + p - LAG
-            pass_on(lax.div(at, n_i), lax.rem(at, n_i))
             send(n + 1, p)
 
     par = (STEPS - 1) % 2

time: 139 us -> 139 us (level)
  no operation moved by 1% of the time
where the time goes in v6:
time: 139 us; the launch traced here: 138 us
  Pallas kernels  138 us (99%)
    pallas_call x1, Pallas kernels, per_device(): pl.pallas_call(functools.partial(kernel, sizes), out_shape=(out, out), in...  134 us
    pallas_call x1, Pallas kernels, per_device(): pl.pallas_call(write_out, out_shape=(out, out), in_specs=[pl.BlockSpec(me...  3.37 us

profile of v6, /device:TPU:96, one launch (start us, length us, event | category | flops | bytes accessed | tf_op | source)
XLA Modules:
  0.0 138.2 jit_solution(13393523167057234478)
XLA Ops:
  0.6 134.2 %transport.1 = (f32[128,8,8,128]{3,2,1,0:T(8,128)S(1)}, f32[128,8,8,128]{3,2,1,0:T(8,128)S(1)}) custom-call(f32[128,8,8,128]{3,2,1,0:T(8,128)} %x_hbm.1, f32[128,8,8,128]{3,2,1,0:T(8,128)} %fj_hbm.1, f32[128,8,8,128]{3,2,1,0:T(8,128)} %fi_hbm.1, f32[128,8,8,128]{3,2,1,0:T(8,128)} %fk_hbm.1), custom_call_target="tpu_custom_call" | custom-call | tf_op jit(solution)/shard_map/transport/pallas_call | solution.py:379
  134.9 3.4 %write_out.1 = (f32[128,8,8,128]{3,2,1,0:T(8,128)}, f32[128,8,8,128]{3,2,1,0:T(8,128)}) custom-call(f32[128,8,8,128]{3,2,1,0:T(8,128)S(1)} %get-tuple-element.4.std, f32[128,8,8,128]{3,2,1,0:T(8,128)S(1)} %get-tuple-element.5.end), custom_call_target="tpu_custom_call" | custom-call | tf_op jit(solution)/shard_map/write_out/pallas_call | solution.py:404

commit v7 on v5

--- a/solution.py
+++ b/solution.py
@@ -151,15 +151,17 @@
         for d in range(2):
             k_out[par, d, p] = rows[par, i + 1, pl.ds(n_k + d * (n_k - 1), n_j, stride=n_k), :]
 
-    def send(n, p):
+    def send_slant(n, p):
+        around = passed(down, p)
+        for d in range(2):
+            @pl.when(jnp.logical_and(slant[d], around))
+            def _():
+                k_slant(n, d, p).start()
+
+    def send_rest(n, p):
         par = lax.rem(n, 2)
         around = passed(down, p)
         for d in range(2):
-            @pl.when(jnp.logical_and(slant[d], around))
-            def _():
-                k_slant(n, d, p).start()
-
-        for d in range(2):
             @pl.when(jnp.logical_and(has[f"k{d}"], jnp.logical_not(jnp.logical_and(slant[d], around))))
             def _():
                 k_copy(par, d, p).start()
@@ -168,6 +170,10 @@
             @pl.when(jnp.logical_and(p == d, has[f"i{d}"]))
             def _():
                 i_copy(par, d).start()
+
+    def send(n, p):
+        send_slant(n, p)
+        send_rest(n, p)
 
     def sent(par, p):
         for d in range(2):
@@ -214,11 +220,16 @@
     def _(p):
         load(0, p).wait()
         extract(0, p)
-        send(0, p)
-
-        @pl.when(p >= FIRST_LAG)
-        def _():
-            pass_on(0, p - FIRST_LAG)
+        send_slant(0, p)
+
+        @pl.when(p <= FIRST_LAG)
+        def _():
+            send_rest(0, p)
+
+    @pl.loop(FIRST_LAG + 1, n_i)
+    def _(p):
+        pass_on(0, p - FIRST_LAG - 1)
+        send_rest(0, p)
 
     @pl.loop(0, n_i)
     def _(p):
@@ -247,7 +258,7 @@
                 for par in range(2):
                     field[par, i + 1, d * (n_j + 1)] = nothing[0]
 
-    @pl.loop(n_i - FIRST_LAG, n_i - LAG)
+    @pl.loop(n_i - FIRST_LAG - 1, n_i - LAG)
     def _(p):
         pass_on(0, p)
 

time: 139 us -> 139 us (level)
  no operation moved by 1% of the time
where the time goes in v7:
time: 139 us; the launch traced here: 138 us
  Pallas kernels  138 us (99%)
    pallas_call x1, Pallas kernels, per_device(): pl.pallas_call(functools.partial(kernel, sizes), out_shape=(out, out), in...  134 us
    pallas_call x1, Pallas kernels, per_device(): pl.pallas_call(write_out, out_shape=(out, out), in_specs=[pl.BlockSpec(me...  3.37 us

profile of v7, /device:TPU:96, one launch (start us, length us, event | category | flops | bytes accessed | tf_op | source)
XLA Modules:
  0.0 138.2 jit_solution(17938780993547784201)
XLA Ops:
  0.6 134.2 %transport.1 = (f32[128,8,8,128]{3,2,1,0:T(8,128)S(1)}, f32[128,8,8,128]{3,2,1,0:T(8,128)S(1)}) custom-call(f32[128,8,8,128]{3,2,1,0:T(8,128)} %x_hbm.1, f32[128,8,8,128]{3,2,1,0:T(8,128)} %fj_hbm.1, f32[128,8,8,128]{3,2,1,0:T(8,128)} %fi_hbm.1, f32[128,8,8,128]{3,2,1,0:T(8,128)} %fk_hbm.1), custom_call_target="tpu_custom_call" | custom-call | tf_op jit(solution)/shard_map/transport/pallas_call | solution.py:390
  134.9 3.4 %write_out.1 = (f32[128,8,8,128]{3,2,1,0:T(8,128)}, f32[128,8,8,128]{3,2,1,0:T(8,128)}) custom-call(f32[128,8,8,128]{3,2,1,0:T(8,128)S(1)} %get-tuple-element.4.std, f32[128,8,8,128]{3,2,1,0:T(8,128)S(1)} %get-tuple-element.5.end), custom_call_target="tpu_custom_call" | custom-call | tf_op jit(solution)/shard_map/write_out/pallas_call | solution.py:415
